TPU v7x, 8 devices: a whole 2x2x1 slice. The times are simulated.
8 devices in a mesh: dp: 2 (over z, y), tp: 4 (over x, core).
Axes of the slice: x: 2, y: 2, z: 1, core: 2. Of those that a mesh axis runs over, the one named last changes fastest.
Arguments:
- start_hidden: bfloat16 [64, 2304], P('dp'), parts along dimension 0
- embedding: bfloat16 [256000, 2304], P('tp')
- pre_norm: bfloat16 [2304], replicated
- w_gate: bfloat16 [2304, 9216], P(None, 'tp')
- w_up: bfloat16 [2304, 9216], P(None, 'tp')
- w_down: bfloat16 [9216, 2304], P('tp')
- post_norm: bfloat16 [2304], replicated
- final_norm: bfloat16 [2304], replicated
- temperature: float32 [], replicated
- step_noise: float32 [4, 64, 256000], P(None, 'dp', 'tp'), parts along dimension 1
Outputs:
- output 1: int32 [4, 64], P(None, 'dp'), parts along dimension 1
- output 2: bfloat16 [64, 2304], P('dp'), parts along dimension 0
There are 2 independent parts. A program takes and returns all parts, laid end to end along the dimension named above; an argument that names none is the same for every part.
All inputs are finite; a program needn't handle non-finite values.
Results may differ from a plain program's by a relative error of at most 0.001.
Values are sent between devices in bfloat16 or wider.
A program may use at most 1.5 GiB of HBM per device.

v0:
```python
import math
import jax
import jax.numpy as jnp
from jax import lax
from jax.sharding import PartitionSpec as P

SOFT_CAP = 30.0
EPSILON = 1e-6


def rms_scale(values, gain_vec):
    x_f32 = values.astype(jnp.float32)
    mean_sq = jnp.mean(x_f32 * x_f32, axis=-1, keepdims=True)
    return x_f32 * lax.rsqrt(mean_sq + EPSILON) * (1.0 + gain_vec.astype(jnp.float32))


def solution(mesh):
    def local_steps(start_hidden, embedding, pre_norm, w_gate, w_up, w_down, post_norm, final_norm, value_a11, step_noise):
        vocab_local = embedding.shape[0]
        row_offset = lax.axis_index('tp') * vocab_local
        embed_scale = jnp.asarray(math.sqrt(embedding.shape[1]), jnp.bfloat16).astype(jnp.float32)
        hidden = start_hidden
        token_list = []
        for step_idx in range(step_noise.shape[0]):
            normed = rms_scale(hidden, pre_norm).astype(jnp.bfloat16)
            gate_proj = jnp.dot(normed, w_gate, preferred_element_type=jnp.float32)
            up_proj = jnp.dot(normed, w_up, preferred_element_type=jnp.float32)
            gated_act = (jax.nn.gelu(gate_proj, approximate=True) * up_proj).astype(jnp.bfloat16)
            down_part = jnp.dot(gated_act, w_down, preferred_element_type=jnp.float32)
            down_sum = lax.psum(down_part, 'tp')
            post_out = rms_scale(down_sum, post_norm).astype(jnp.bfloat16)
            resid_sum = (hidden.astype(jnp.float32) + post_out.astype(jnp.float32)).astype(jnp.bfloat16)
            final_in = rms_scale(resid_sum, final_norm).astype(jnp.bfloat16)
            logits = lax.dot_general(final_in, embedding, (((1,), (1,)), ((), ())), preferred_element_type=jnp.float32)
            scores = SOFT_CAP * jnp.tanh(logits / SOFT_CAP) / value_a11 + step_noise[step_idx]
            local_best = jnp.max(scores, axis=1)
            local_arg = jnp.argmax(scores, axis=1)
            global_id = (local_arg + row_offset).astype(jnp.float32)
            pair_all = lax.all_gather(jnp.stack([local_best, global_id]), 'tp')
            win_shard = jnp.argmax(pair_all[:, 0, :], axis=0)
            next_token = jnp.take_along_axis(pair_all[:, 1, :], win_shard[None, :], axis=0)[0].astype(jnp.int32)
            local_row = next_token - row_offset
            owned = (local_row >= 0) & (local_row < vocab_local)
            picked = jnp.take(embedding, jnp.clip(local_row, 0, vocab_local - 1), axis=0)
            picked = jnp.where(owned[:, None], picked, jnp.zeros_like(picked))
            looked_up = lax.psum(picked, 'tp')
            hidden = (looked_up.astype(jnp.float32) * embed_scale).astype(jnp.bfloat16)
            token_list.append(next_token)
        return jnp.stack(token_list), hidden

    return jax.shard_map(local_steps, mesh=mesh, in_specs=(P('dp', None), P('tp', None), P(), P(None, 'tp'), P(None, 'tp'), P('tp', None), P(), P(), P(), P(None, 'dp', 'tp')), out_specs=(P(None, 'dp'), P('dp', None)), check_vma=False)
```

profile of v0, /device:TPU:0, one launch (start us, length us, event | category | flops | bytes accessed | tf_op | source)
XLA Modules:
  0.0 819.3 jit_solution(11768205554368888193)
XLA Ops:
  9.0 6.1 fusion.118
  15.1 11.3 %fusion.27 = f32[32,2304]{1,0:T(8,128)} fusion(bf16[2304,2304]{1,0:T(8,128)(2,1)} %param.19, bf16[2304,2304]{1,0:T(8,128)(2,1)} %param.18, f32[32,2304]{1,0:T(8,128)S(1)} %fusion.118, bf16[32,2304]{1,0:T(8,128)(2,1)S(1)} %copy-done, f32[2304]{0:T(1024)S(1)} %convert_add_fusion.6, f32[32]{0:T(128)S(1)} %add_rsqrt_fusion.11), kind=kOutput, calls=%fused_computation.43 | convolution fusion | flops 680509440 | bytes 21980288 | tf_op jit(solution)/shard_map/dot_general | solution.py:29
  27.2 29.0 %all-reduce.9.cloned.1.call-done = f32[32,2304]{1,0:T(8,128)} async-done(((f32[32,2304]{1,0:T(8,128)}), f32[32,2304]{1,0:T(8,128)}) %all-reduce.9.cloned.1.call-update) | async-done | bytes 294928 | tf_op jit(solution)/shard_map/psum | solution.py:30
  57.3 1.2 fusion.28
  58.5 112.5 %fusion.19 = (f32[32]{0:T(128)S(1)}, s32[32]{0:T(128)S(1)}) fusion(bf16[64000,2304]{1,0:T(8,128)(2,1)} %param.15, f32[4,32,64000]{2,1,0:T(8,128)} %param.23, f32[]{:T(128)S(6)} %copy.20, bf16[32,2304]{1,0:T(8,128)(2,1)S(1)} %get-tuple-element.55, f32[2304]{0:T(1024)S(1)} %convert_add_fusion.4, f32[32]{0:T(128)S(1)} %add_rsqrt_fusion.9), kind=kOutput, calls=%fused_computation.31 | convolution fusion | flops 9464102912 | bytes 303261056 | tf_op jit(solution)/shard_map/dot_general | solution.py:34
  171.0 6.5 all-gather.4
  179.3 1.8 gather_fusion.1
  182.1 28.8 %all-reduce.11.cloned.1.call-done = bf16[32,2304]{1,0:T(8,128)(2,1)} async-done(((bf16[32,2304]{1,0:T(8,128)(2,1)}), bf16[32,2304]{1,0:T(8,128)(2,1)}) %all-reduce.11.cloned.1.call-update) | async-done | bytes 147472 | tf_op jit(solution)/shard_map/psum | solution.py:46
  212.1 6.1 fusion.130
  218.2 11.3 %fusion.26 = f32[32,2304]{1,0:T(8,128)} fusion(bf16[2304,2304]{1,0:T(8,128)(2,1)} %param.19, bf16[2304,2304]{1,0:T(8,128)(2,1)} %param.18, f32[32,2304]{1,0:T(8,128)S(1)} %fusion.130, f32[32]{0:T(128)S(1)} %add_rsqrt_fusion.8, f32[2304]{0:T(1024)S(1)} %convert_add_fusion.6, bf16[32,2304]{1,0:T(8,128)(2,1)S(1)} %copy-done.2), kind=kOutput, calls=%fused_computation.42 | convolution fusion | flops 680730624 | bytes 21980288 | tf_op jit(solution)/shard_map/dot_general | solution.py:29
  229.6 27.0 %all-reduce.13.cloned.1.call-done = f32[32,2304]{1,0:T(8,128)} async-done(((f32[32,2304]{1,0:T(8,128)}), f32[32,2304]{1,0:T(8,128)}) %all-reduce.13.cloned.1.call-update) | async-done | bytes 294928 | tf_op jit(solution)/shard_map/psum | solution.py:30
  258.9 112.4 %fusion.14 = (f32[32]{0:T(128)S(1)}, s32[32]{0:T(128)S(1)}) fusion(bf16[64000,2304]{1,0:T(8,128)(2,1)} %param.15, f32[4,32,64000]{2,1,0:T(8,128)} %param.23, f32[]{:T(128)S(6)} %copy.20, bf16[32,2304]{1,0:T(8,128)(2,1)S(1)} %get-tuple-element.49, f32[32]{0:T(128)S(1)} %add_rsqrt_fusion.6, f32[2304]{0:T(1024)S(1)} %convert_add_fusion.4), kind=kOutput, calls=%fused_computation.25 | convolution fusion | flops 9464102912 | bytes 303261056 | tf_op jit(solution)/shard_map/dot_general | solution.py:34
  371.3 6.5 all-gather.5
  379.7 1.9 gather_fusion.3
  382.4 28.9 %all-reduce.15.cloned.1.call-done = bf16[32,2304]{1,0:T(8,128)(2,1)} async-done(((bf16[32,2304]{1,0:T(8,128)(2,1)}), bf16[32,2304]{1,0:T(8,128)(2,1)}) %all-reduce.15.cloned.1.call-update) | async-done | bytes 147472 | tf_op jit(solution)/shard_map/psum | solution.py:46
  412.5 6.1 fusion.126
  418.6 11.3 %fusion.25 = f32[32,2304]{1,0:T(8,128)} fusion(bf16[2304,2304]{1,0:T(8,128)(2,1)} %param.19, bf16[2304,2304]{1,0:T(8,128)(2,1)} %param.18, f32[32,2304]{1,0:T(8,128)S(1)} %fusion.126, f32[32]{0:T(128)S(1)} %add_rsqrt_fusion.5, f32[2304]{0:T(1024)S(1)} %convert_add_fusion.6, bf16[32,2304]{1,0:T(8,128)(2,1)S(1)} %copy-done.3), kind=kOutput, calls=%fused_computation.41 | convolution fusion | flops 680730624 | bytes 21980288 | tf_op jit(solution)/shard_map/dot_general | solution.py:29
  430.2 26.8 %all-reduce.17.cloned.1.call-done = f32[32,2304]{1,0:T(8,128)} async-done(((f32[32,2304]{1,0:T(8,128)}), f32[32,2304]{1,0:T(8,128)}) %all-reduce.17.cloned.1.call-update) | async-done | bytes 294928 | tf_op jit(solution)/shard_map/psum | solution.py:30
  458.1 1.2 fusion.34
  459.3 112.4 %fusion.9 = (f32[32]{0:T(128)S(1)}, s32[32]{0:T(128)S(1)}) fusion(bf16[64000,2304]{1,0:T(8,128)(2,1)} %param.15, f32[4,32,64000]{2,1,0:T(8,128)} %param.23, f32[]{:T(128)S(6)} %copy.20, bf16[32,2304]{1,0:T(8,128)(2,1)S(1)} %get-tuple-element.43, f32[32]{0:T(128)S(1)} %add_rsqrt_fusion.3, f32[2304]{0:T(1024)S(1)} %convert_add_fusion.4), kind=kOutput, calls=%fused_computation.19 | convolution fusion | flops 9464102912 | bytes 303261056 | tf_op jit(solution)/shard_map/dot_general | solution.py:34
  571.7 6.5 all-gather.6
  579.6 1.8 gather_fusion.5
  582.2 28.9 %all-reduce.19.cloned.1.call-done = bf16[32,2304]{1,0:T(8,128)(2,1)} async-done(((bf16[32,2304]{1,0:T(8,128)(2,1)}), bf16[32,2304]{1,0:T(8,128)(2,1)}) %all-reduce.19.cloned.1.call-update) | async-done | bytes 147472 | tf_op jit(solution)/shard_map/psum | solution.py:46
  612.3 6.1 fusion.122
  618.4 11.3 %fusion.24 = f32[32,2304]{1,0:T(8,128)} fusion(bf16[2304,2304]{1,0:T(8,128)(2,1)} %param.19, bf16[2304,2304]{1,0:T(8,128)(2,1)} %param.18, f32[32,2304]{1,0:T(8,128)S(1)} %fusion.122, f32[32]{0:T(128)S(1)} %add_rsqrt_fusion.2, f32[2304]{0:T(1024)S(1)} %convert_add_fusion.6, bf16[32,2304]{1,0:T(8,128)(2,1)S(1)} %copy-done.1), kind=kOutput, calls=%fused_computation.40 | convolution fusion | flops 680730624 | bytes 21980288 | tf_op jit(solution)/shard_map/dot_general | solution.py:29
  629.7 27.0 %all-reduce.21.cloned.1.call-done = f32[32,2304]{1,0:T(8,128)} async-done(((f32[32,2304]{1,0:T(8,128)}), f32[32,2304]{1,0:T(8,128)}) %all-reduce.21.cloned.1.call-update) | async-done | bytes 294928 | tf_op jit(solution)/shard_map/psum | solution.py:30
  657.8 1.2 fusion.37
  659.1 112.4 %fusion.4 = (f32[32]{0:T(128)S(1)}, s32[32]{0:T(128)S(1)}) fusion(bf16[64000,2304]{1,0:T(8,128)(2,1)} %param.15, f32[4,32,64000]{2,1,0:T(8,128)} %param.23, f32[]{:T(128)S(6)} %copy.20, bf16[32,2304]{1,0:T(8,128)(2,1)S(1)} %get-tuple-element.37, f32[32]{0:T(128)S(1)} %add_rsqrt_fusion, f32[2304]{0:T(1024)S(1)} %convert_add_fusion.4), kind=kOutput, calls=%fused_computation.13 | convolution fusion | flops 9464102912 | bytes 303261056 | tf_op jit(solution)/shard_map/dot_general | solution.py:34
  771.6 6.5 all-gather.7
  779.4 1.8 gather_fusion.7
  782.6 28.2 %all-reduce.23.cloned.1.call-done = bf16[32,2304]{1,0:T(8,128)(2,1)} async-done(((bf16[32,2304]{1,0:T(8,128)(2,1)}), bf16[32,2304]{1,0:T(8,128)(2,1)}) %all-reduce.23.cloned.1.call-update) | async-done | bytes 147472 | tf_op jit(solution)/shard_map/psum | solution.py:46
  810.8 1.6 multiply_convert_fusion
  (110 shorter events, 21.8 us)
Async XLA Ops:
  7.2 8.0 copy-start
  7.2 49.0 %all-reduce.9.cloned.1.call-start = ((), (), s32[]{:S(2)}) async-start(), calls=%async_computation | async-start | bytes 589824 | tf_op jit(solution)/shard_map/psum | solution.py:30
  15.1 12.0 %copy-start.4 = (bf16[2304]{0:T(1024)(128)(2,1)S(1)}, bf16[2304]{0:T(1024)(128)(2,1)}, u32[]{:S(2)}) copy-start(bf16[2304]{0:T(1024)(128)(2,1)} %param.20) | copy-start | bytes 13828
  15.1 12.1 %copy-start.5 = (bf16[2304]{0:T(1024)(128)(2,1)S(1)}, bf16[2304]{0:T(1024)(128)(2,1)}, u32[]{:S(2)}) copy-start(bf16[2304]{0:T(1024)(128)(2,1)} %param.21) | copy-start | bytes 13828
  26.5 184.5 %all-reduce.11.cloned.1.call-start = ((), (), s32[]{:S(2)}) async-start(), calls=%async_computation.1 | async-start | bytes 294912 | tf_op jit(solution)/shard_map/psum | solution.py:46
  178.8 0.5 copy-start.6
  181.9 74.7 %all-reduce.13.cloned.1.call-start = ((), (), s32[]{:S(2)}) async-start(), calls=%async_computation.2 | async-start | bytes 589824 | tf_op jit(solution)/shard_map/psum | solution.py:30
  210.9 7.3 copy-start.2
  229.5 181.8 %all-reduce.15.cloned.1.call-start = ((), (), s32[]{:S(2)}) async-start(), calls=%async_computation.3 | async-start | bytes 294912 | tf_op jit(solution)/shard_map/psum | solution.py:46
  379.1 0.6 copy-start.8
  382.4 74.6 %all-reduce.17.cloned.1.call-start = ((), (), s32[]{:S(2)}) async-start(), calls=%async_computation.4 | async-start | bytes 589824 | tf_op jit(solution)/shard_map/psum | solution.py:30
  411.4 7.3 copy-start.3
  429.9 181.2 %all-reduce.19.cloned.1.call-start = ((), (), s32[]{:S(2)}) async-start(), calls=%async_computation.5 | async-start | bytes 294912 | tf_op jit(solution)/shard_map/psum | solution.py:46
  582.2 74.6 %all-reduce.21.cloned.1.call-start = ((), (), s32[]{:S(2)}) async-start(), calls=%async_computation.6 | async-start | bytes 589824 | tf_op jit(solution)/shard_map/psum | solution.py:30
  611.1 7.3 copy-start.1
  629.7 181.1 %all-reduce.23.cloned.1.call-start = ((), (), s32[]{:S(2)}) async-start(), calls=%async_computation.7 | async-start | bytes 294912 | tf_op jit(solution)/shard_map/psum | solution.py:46
  659.1 123.0 %copy-start.7 = (s32[1,32]{1,0:T(1,128)S(1)}, s32[1,32]{1,0:T(1,128)}, u32[]{:S(2)}) copy-start(s32[1,32]{1,0:T(1,128)} %copy-done.6) | copy-start | bytes 388
  659.1 123.0 %copy-start.9 = (s32[1,32]{1,0:T(1,128)S(1)}, s32[1,32]{1,0:T(1,128)}, u32[]{:S(2)}) copy-start(s32[1,32]{1,0:T(1,128)} %copy-done.8) | copy-start | bytes 388
Sparse Core Ops, SparseCore 0:
  26.6 29.5 all-reduce.8
  182.0 28.8 all-reduce.10
  229.6 26.8 all-reduce.12
  382.5 28.8 all-reduce.14
  430.0 26.8 all-reduce.16
  582.3 28.7 all-reduce.18
  629.8 26.8 all-reduce.20
  782.1 28.6 all-reduce.22
where the time goes:
time: 823 us; the launch traced here: 819 us
  matrix products  519 us (63%)
  waiting for transfers between devices  225 us (27%)
  blocking collectives  25.9 us (3%)
  other arithmetic  22.1 us (3%)
  between operations  15.1 us (2%)
  local copies, waits for them, and re-layouts  11.5 us (1%)
    dot_general x4, matrix products, local_steps(): lax.dot_general(final_in, embedding, (((1,), (1,)), ((), ())), preferred_...  450 us
    psum x4, waiting for transfers between devices, local_steps(): looked_up = lax.psum(picked, 'tp')  115 us
    psum x4, waiting for transfers between devices, local_steps(): down_sum = lax.psum(down_part, 'tp')  110 us
    dot_general x4, matrix products, local_steps(): down_part = jnp.dot(gated_act, w_down, preferred_element_type=jnp.float32)  45.2 us
    all_gather x4, blocking collectives, local_steps(): pair_all = lax.all_gather(jnp.stack([local_best, global_id]), 'tp')  25.9 us
    dot_general x4, matrix products, local_steps(): gate_proj = jnp.dot(normed, w_gate, preferred_element_type=jnp.float32)  24.4 us
  transfers between devices with their start and end apart: 8, of which 8 were waited for; matrix products, arithmetic and copies ran while one was open for 0% of the time, Pallas kernels for 0%

commit v1 on v0

v1 whole, which is shorter than its diff:
```python
import functools
import math

import jax
import jax.numpy as jnp
import numpy as np
from jax import lax
from jax.experimental import pallas as pl
from jax.experimental.pallas import tpu as pltpu
from jax.sharding import PartitionSpec as P

SOFT_CAP = 30.0
EPSILON = 1e-6
MESH = pl.DeviceIdType.MESH

SUB = 512
NSUB = 5
GROUP = SUB * NSUB
RING_GROUPS = 4
OWN = 5
NEG = -3.0e38


def rms_scale(x_f32, gain_row):
    mean_sq = jnp.mean(x_f32 * x_f32, axis=-1, keepdims=True)
    return x_f32 * lax.rsqrt(mean_sq + EPSILON) * (1.0 + gain_row.astype(jnp.float32))


def remote(src, dst, sem, peer):
    return pltpu.make_async_remote_copy(
        src_ref=src, dst_ref=dst, send_sem=sem.at[0], recv_sem=sem.at[1], device_id=peer, device_id_type=MESH
    )


def step_kernel(cfg, *refs):
    step, first, last, n_group, embed_scale = cfg
    refs = list(refs)
    take = lambda n: [refs.pop(0) for _ in range(n)]
    if first:
        (hid_ref,) = take(1)
    else:
        rows_ref, meta_ref = take(2)
    if not last:
        pre_ref, post_ref, fin_ref, temp_ref, wg_ref, wu_ref, wd_ref, emb_ref, noise_ref = take(9)
    if not first:
        tok_ref, hout_ref = take(2)
    if not last:
        best_ref = take(1)[0]
    if not first:
        rows_a, meta_a, rows_m, meta_m, rows_b, meta_b, rows_f, meta_f, rows_c, meta_c, sem_rows, sem_meta = take(12)
    if not last:
        (ring, nz_own, nz_oth, part_s, part_a, half_s, part_b, f_send, f_all, f_own, f_oth, f_two,
         hid32, gate_s, bv, bi, best_oth, best_in,
         sem_w, sem_e, sem_no, sem_ns, sem_nr, sem_ra, sem_rb, sem_f, sem_fo, sem_by) = take(28)

    dp, tp = lax.axis_index("dp"), lax.axis_index("tp")
    core, chip = lax.rem(tp, 2), lax.div(tp, 2)
    tp_sib = chip * 2 + (1 - core)
    tp_x = (1 - chip) * 2 + core
    tp_diag = (1 - chip) * 2 + (1 - core)
    sib, over, diag, pair = (dp, tp_sib), (dp, tp_x), (dp, tp_diag), (1 - dp, tp)

    if not last:
        half = (n_group - OWN) // 2
        n_iter = OWN + half
        width = ring.shape[1]
        inner = wg_ref.shape[1]
        w_copies = [
            pltpu.make_async_copy(wg_ref, ring.at[pl.ds(0, width)], sem_w.at[0]),
            pltpu.make_async_copy(wu_ref, ring.at[pl.ds(width, width)], sem_w.at[1]),
            pltpu.make_async_copy(wd_ref, ring.at[pl.ds(2 * width, inner)], sem_w.at[2]),
        ]

        def e_copy(i, j):
            group = i + jnp.where(i < OWN, 0, dp * half)
            slot = lax.rem(i + 3, RING_GROUPS)
            return pltpu.make_async_copy(
                emb_ref.at[pl.ds(group * GROUP + j * SUB, SUB)],
                ring.at[pl.ds(slot * GROUP + j * SUB, SUB)],
                sem_e.at[slot, j],
            )

        def e_start(i):
            for j in range(NSUB):
                e_copy(i, j).start()

        def no_copy(i):
            group = i + jnp.where(i < OWN, 0, dp * half)
            return pltpu.make_async_copy(
                noise_ref.at[step, :, pl.ds(group * GROUP, GROUP)], nz_own.at[i], sem_no.at[i]
            )

        def nr_copy(j):
            group = OWN + (1 - dp) * half + j
            return pltpu.make_async_remote_copy(
                src_ref=noise_ref.at[step, :, pl.ds(group * GROUP, GROUP)],
                dst_ref=nz_oth.at[j],
                send_sem=sem_ns.at[j],
                recv_sem=sem_nr.at[j],
                device_id=pair,
                device_id_type=MESH,
            )

        for copy in w_copies:
            copy.start()
        e_start(0)
        pl.loop(0, n_iter)(lambda i: no_copy(i).start())

    barrier = pltpu.get_barrier_semaphore()
    peers = (sib, over) if last else (sib, over, diag, pair)
    for peer in peers:
        pl.semaphore_signal(barrier, inc=1, device_id=peer, device_id_type=MESH)
    pl.semaphore_wait(barrier, len(peers))

    if not last:
        early = 3
        pl.loop(0, early)(lambda j: nr_copy(j).start())

    if first:
        hid = hid_ref[...].astype(jnp.float32)
    else:
        a_rows = remote(rows_ref.at[1 - core], rows_a, sem_rows.at[0], sib)
        a_meta = remote(meta_ref.at[1 - core], meta_a, sem_meta.at[0], sib)
        a_rows.start()
        a_meta.start()
        a_rows.wait()
        a_meta.wait()
        mine = meta_ref[core]
        seen = meta_a[...]
        keep = mine[0] >= seen[0]
        meta_m[...] = jnp.where(keep[None], mine, seen)
        rows_m[...] = jnp.where(
            keep[:, :1], rows_ref[core].astype(jnp.float32), rows_a[...].astype(jnp.float32)
        ).astype(jnp.bfloat16)
        b_rows = remote(rows_m, rows_b, sem_rows.at[1], over)
        b_meta = remote(meta_m, meta_b, sem_meta.at[1], over)
        b_rows.start()
        b_meta.start()
        b_rows.wait()
        b_meta.wait()
        mine = meta_m[...]
        seen = meta_b[...]
        keep = mine[0] >= seen[0]
        meta_f[...] = jnp.where(keep[None], mine, seen)
        rows_f[...] = jnp.where(
            keep[:, :1], rows_m[...].astype(jnp.float32), rows_b[...].astype(jnp.float32)
        ).astype(jnp.bfloat16)
        c_rows = remote(rows_f, rows_c, sem_rows.at[2], sib)
        c_meta = remote(meta_f, meta_c, sem_meta.at[2], sib)
        c_rows.start()
        c_meta.start()
        c_rows.wait()
        c_meta.wait()
        low = core == 0
        r_f, r_c = rows_f[...].astype(jnp.float32), rows_c[...].astype(jnp.float32)
        t_f, t_c = meta_f[1], meta_c[1]
        picked = jnp.concatenate([jnp.where(low, r_f, r_c), jnp.where(low, r_c, r_f)], axis=0)
        tok_ref[...] = jnp.concatenate([jnp.where(low, t_f, t_c), jnp.where(low, t_c, t_f)], axis=0).astype(jnp.int32)
        hid_bf = (picked * embed_scale).astype(jnp.bfloat16)
        hout_ref[...] = hid_bf
        hid = hid_bf.astype(jnp.float32)

    if last:
        return

    batch = hid.shape[0]
    quarter = batch // 4
    hid32[...] = hid.reshape(4, quarter, width)
    normed = rms_scale(hid, pre_ref[...]).astype(jnp.bfloat16)
    f_two[pl.ds(0, batch)] = normed
    w_copies[0].wait()
    w_copies[1].wait()
    col = 768

    @pl.loop(0, inner // col)
    def _(n):
        cols = pl.ds(pl.multiple_of(n * col, col), col)
        lhs = f_two[pl.ds(0, batch)]
        gate = jnp.dot(lhs, ring[pl.ds(0, width), cols], preferred_element_type=jnp.float32)
        up = jnp.dot(lhs, ring[pl.ds(width, width), cols], preferred_element_type=jnp.float32)
        gate_s[:, cols] = (jax.nn.gelu(gate, approximate=True) * up).astype(jnp.bfloat16)

    e_start(1)
    w_copies[2].wait()

    @pl.loop(0, width // col)
    def _(n):
        cols = pl.ds(pl.multiple_of(n * col, col), col)
        part_s[:, :, cols] = jnp.dot(
            gate_s[...], ring[pl.ds(2 * width, inner), cols], preferred_element_type=jnp.float32
        ).reshape(4, quarter, col)

    e_start(2)
    e_start(3)

    ra = remote(part_s.at[pl.ds(2 * (1 - core), 2)], part_a, sem_ra, sib)
    ra.start()
    ra.wait()
    half_s[...] = part_s[pl.ds(2 * core, 2)] + part_a[...]
    rb = remote(half_s.at[1 - chip], part_b, sem_rb, over)
    rb.start()
    rb.wait()
    down_sum = half_s[chip] + part_b[...]
    place = 2 * core + chip
    post_out = rms_scale(down_sum, post_ref[...]).astype(jnp.bfloat16)
    resid = (hid32[place] + post_out.astype(jnp.float32)).astype(jnp.bfloat16)
    final_in = rms_scale(resid.astype(jnp.float32), fin_ref[...]).astype(jnp.bfloat16)
    f_send[...] = final_in
    f_copies = [remote(f_send, f_all.at[k], sem_f.at[k], peer) for k, peer in enumerate((sib, over, diag))]
    for copy in f_copies:
        copy.start()
    for copy in f_copies:
        copy.wait()
    me_f, sib_f, over_f, diag_f = (v.astype(jnp.float32) for v in (f_send[...], f_all[0], f_all[1], f_all[2]))
    low_core, low_chip = core == 0, chip == 0
    core0 = [jnp.where(low_core, a, b) for a, b in ((me_f, sib_f), (over_f, diag_f))]
    core1 = [jnp.where(low_core, b, a) for a, b in ((me_f, sib_f), (over_f, diag_f))]
    order = [
        jnp.where(low_chip, core0[0], core0[1]),
        jnp.where(low_chip, core0[1], core0[0]),
        jnp.where(low_chip, core1[0], core1[1]),
        jnp.where(low_chip, core1[1], core1[0]),
    ]
    f_bf = jnp.concatenate(order, axis=0).astype(jnp.bfloat16)
    f_own[...] = f_bf
    f_two[pl.ds(0, batch)] = f_bf
    fo = remote(f_own, f_oth, sem_fo, pair)
    fo.start()
    pl.loop(early, half)(lambda j: nr_copy(j).start())

    bv[...] = jnp.full_like(bv, NEG)
    bi[...] = jnp.zeros_like(bi)
    c1 = temp_ref[0:1, 0:1]
    c2 = temp_ref[1:2, 0:1]

    def score(i, rows, nz_refs):
        slot = lax.rem(i + 3, RING_GROUPS)
        group = i + jnp.where(i < OWN, 0, dp * half)
        for j in range(NSUB):
            e_copy(i, j).wait()
        lhs = f_two[pl.ds(0, rows)]
        for j in range(NSUB):
            block = ring[pl.ds(pl.multiple_of(slot * GROUP + j * SUB, SUB), SUB), :]
            z = lax.dot_general(lhs, block, (((1,), (1,)), ((), ())), preferred_element_type=jnp.float32)
            s = jnp.tanh(z * (1.0 / SOFT_CAP)) * c1 * c2
            for part, nz in enumerate(nz_refs):
                take_rows = pl.ds(part * batch, batch)
                for q in range(SUB // 256):
                    v = s[part * batch : (part + 1) * batch, q * 256 : (q + 1) * 256]
                    v = v + nz[:, j * SUB + q * 256 : j * SUB + (q + 1) * 256]
                    old = bv[take_rows]
                    better = v > old
                    bv[take_rows] = jnp.where(better, v, old)
                    bi[take_rows] = jnp.where(better, group * (GROUP // 256) + (j * (SUB // 256) + q), bi[take_rows])

        @pl.when(i + RING_GROUPS < n_iter)
        def _():
            e_start(i + RING_GROUPS)

    @pl.loop(0, OWN)
    def _(i):
        no_copy(i).wait()
        score(i, batch, [nz_own.at[i]])

    fo.wait()
    f_two[pl.ds(batch, batch)] = f_oth[...]

    @pl.loop(OWN, n_iter)
    def _(i):
        no_copy(i).wait()
        nr_copy(i - OWN).wait_recv()
        score(i, 2 * batch, [nz_own.at[i], nz_oth.at[i - OWN]])

    pl.loop(0, half)(lambda j: nr_copy(j).wait_send())

    def settle(part):
        val = bv[pl.ds(part * batch, batch)]
        tile = bi[pl.ds(part * batch, batch)]
        top = jnp.max(val, axis=1, keepdims=True)
        ids = (tile * 256 + lax.broadcasted_iota(jnp.int32, tile.shape, 1)).astype(jnp.float32)
        row = jnp.min(jnp.where(val == top, ids, 3.0e7), axis=1, keepdims=True)
        return jnp.broadcast_to(top, (batch, 128)), jnp.broadcast_to(row, (batch, 128))

    o_val, o_row = settle(1)
    best_oth[0] = o_val
    best_oth[1] = o_row
    by = remote(best_oth, best_in, sem_by, pair)
    by.start()
    m_val, m_row = settle(0)
    by.wait()
    keep = m_val >= best_in[0]
    best_ref[0] = jnp.where(keep, m_val, best_in[0])
    best_ref[1] = jnp.where(keep, m_row, best_in[1])


def call_step(step, steps, batch, width, inner, vocab_local, embed_scale, operands):
    first, last = step == 0, step == steps
    f32, bf16, i32 = jnp.float32, jnp.bfloat16, jnp.int32
    vmem, hbm = pl.BlockSpec(memory_space=pltpu.VMEM), pl.BlockSpec(memory_space=pl.ANY)
    dma = pltpu.SemaphoreType.DMA
    n_group = vocab_local // GROUP
    half = (n_group - OWN) // 2
    n_iter = OWN + half
    hb, quarter = batch // 2, batch // 4
    in_specs = [vmem] * (1 if first else 2)
    if not last:
        in_specs += [vmem] * 4 + [hbm] * 5
    outs, scratch = [], []
    if not first:
        outs += [jax.ShapeDtypeStruct((batch, 128), i32), jax.ShapeDtypeStruct((batch, width), bf16)]
        rows, meta = pltpu.VMEM((hb, width), bf16), pltpu.VMEM((2, hb, 128), f32)
        scratch += [rows, meta] * 5 + [dma((3, 2)), dma((3, 2))]
    if not last:
        outs += [jax.ShapeDtypeStruct((2, batch, 128), f32)]
        scratch += [
            pltpu.VMEM((RING_GROUPS * GROUP, width), bf16),
            pltpu.VMEM((n_iter, batch, GROUP), f32),
            pltpu.VMEM((half, batch, GROUP), f32),
            pltpu.VMEM((4, quarter, width), f32),
            pltpu.VMEM((2, quarter, width), f32),
            pltpu.VMEM((2, quarter, width), f32),
            pltpu.VMEM((quarter, width), f32),
            pltpu.VMEM((quarter, width), bf16),
            pltpu.VMEM((3, quarter, width), bf16),
            pltpu.VMEM((batch, width), bf16),
            pltpu.VMEM((batch, width), bf16),
            pltpu.VMEM((2 * batch, width), bf16),
            pltpu.VMEM((4, quarter, width), f32),
            pltpu.VMEM((batch, inner), bf16),
            pltpu.VMEM((2 * batch, 256), f32),
            pltpu.VMEM((2 * batch, 256), i32),
            pltpu.VMEM((2, batch, 128), f32),
            pltpu.VMEM((2, batch, 128), f32),
            dma((3,)),
            dma((RING_GROUPS, NSUB)),
            dma((n_iter,)),
            dma((half,)),
            dma((half,)),
            dma((2,)),
            dma((2,)),
            dma((3, 2)),
            dma((2,)),
            dma((2,)),
        ]
    return pl.pallas_call(
        functools.partial(step_kernel, (step, first, last, n_group, embed_scale)),
        out_shape=outs,
        in_specs=in_specs,
        out_specs=[vmem] * len(outs),
        scratch_shapes=scratch,
        compiler_params=pltpu.CompilerParams(
            collective_id=step, has_side_effects=True, vmem_limit_bytes=66_000_000 if not last else 16_000_000
        ),
        name=f"step{step}",
    )(*operands)


def solution(mesh):
    def local_steps(start_hidden, embedding, pre_norm, w_gate, w_up, w_down, post_norm, final_norm, temperature, step_noise):
        vocab_local, width = embedding.shape
        batch, steps = start_hidden.shape[0], step_noise.shape[0]
        inner = w_gate.shape[1]
        row_offset = (lax.axis_index("tp") * vocab_local).astype(jnp.float32)
        embed_scale = float(np.float64(math.sqrt(width)).astype(jnp.bfloat16))
        a = jnp.where(temperature > 2.0**64, 2.0**-64, 1.0).astype(jnp.float32)
        temp = jnp.broadcast_to(jnp.stack([SOFT_CAP * a, 1.0 / (temperature * a)])[:, None], (2, 128))
        norms = [v[None] for v in (pre_norm, post_norm, final_norm)]
        common = [*norms, temp, w_gate, w_up, w_down, embedding, step_noise]
        sizes = (steps, batch, width, inner, vocab_local, embed_scale)
        (best,) = call_step(0, *sizes, [start_hidden, *common])
        token_list = []
        for step in range(1, steps + 1):
            local_row = best[1, :, 0].astype(jnp.int32)
            rows = jnp.take(embedding, local_row, axis=0, mode="clip").reshape(2, batch // 2, width)
            meta = jnp.stack([best[0], best[1] + row_offset]).reshape(2, 2, batch // 2, 128).transpose(1, 0, 2, 3)
            outs = call_step(step, *sizes, [rows, meta, *(common if step < steps else [])])
            token_list.append(outs[0][:, 0])
            hidden = outs[1]
            if step < steps:
                best = outs[2]
        return jnp.stack(token_list), hidden

    return jax.shard_map(
        local_steps,
        mesh=mesh,
        in_specs=(P("dp", None), P("tp", None), P(), P(None, "tp"), P(None, "tp"), P("tp", None), P(), P(), P(), P(None, "dp", "tp")),
        out_specs=(P(None, "dp"), P("dp", None)),
        check_vma=False,
    )
```

time: 823 us -> 382 us (0.46)
  matrix products: 519 us -> 0 us
  Pallas kernels: 0 us -> 353 us
  waiting for transfers between devices: 225 us -> 0 us
  blocking collectives: 25.9 us -> 0 us
  between operations: 15.1 us -> 1.4 us
  other arithmetic: 22.1 us -> 8.83 us
    dot_general x12 -> x0, matrix products: 519 us -> none  [the longest x4 450 us: local_steps(): lax.dot_general(final_in, embedding, (((1,), (1,)), ((), ())), preferred_...]
    pallas_call x0 -> x5, Pallas kernels: none -> 353 us  [call_step(): pl.pallas_call(functools.partial(step_kernel, (step, first, last, n_group...]
    psum x8 -> x0, waiting for transfers between devices: 225 us -> none  [the longest x4 115 us: local_steps(): looked_up = lax.psum(picked, 'tp')]
    all_gather x4 -> x0, blocking collectives: 25.9 us -> none  [local_steps(): pair_all = lax.all_gather(jnp.stack([local_best, global_id]), 'tp')]
    reduce_sum x12 -> x0, other arithmetic: 13.6 us -> none  [rms_scale(): mean_sq = jnp.mean(x_f32 * x_f32, axis=-1, keepdims=True)]
  transfers between devices with their start and end apart: 8 -> 0, of which waited for: 8 -> 0; matrix products, arithmetic and copies ran while one was open for 0% -> 0% of each run, Pallas kernels for 0% -> 0%
where the time goes in v1:
time: 382 us; the launch traced here: 380 us
  Pallas kernels  353 us (92%)
  local copies, waits for them, and re-layouts  17.1 us (4%)
  other arithmetic  8.83 us (2%)
    pallas_call x5, Pallas kernels, call_step(): pl.pallas_call(functools.partial(step_kernel, (step, first, last, n_group...  353 us
    gather x4, local copies, waits for them, and re-layouts, local_steps(): jnp.take(embedding, local_row, axis=0, mode='clip')  8.83 us

profile of v1, /device:TPU:0, one launch (start us, length us, event | category | flops | bytes accessed | tf_op | source)
XLA Modules:
  0.0 380.0 jit_solution(10251005674196221870)
XLA Ops:
  1.3 0.1 pad_maximum_fusion
  1.4 0.6 broadcast_in_dim.23.refs_4_.refs_5_
  2.0 1.3 broadcast_in_dim.20.refs_1_.refs_2_
  3.3 1.3 broadcast_in_dim.21.refs_2_.refs_3_
  4.6 1.3 broadcast_in_dim.22.refs_3_.refs_4_
  5.9 87.8 %step0.1 = f32[2,32,128]{2,1,0:T(8,128)} custom-call(bf16[32,2304]{1,0:T(8,128)(2,1)} %refs_0_.1, bf16[1,2304]{1,0:T(2,128)(2,1)} %broadcast_in_dim.20.refs_1_.refs_2_, bf16[1,2304]{1,0:T(2,128)(2,1)} %broadcast_in_dim.21.refs_2_.refs_3_, bf16[1,2304]{1,0:T(2,128)(2,1)} %broadcast_in_dim.22.refs_3_.refs_4_, f32[2,128]{1,0:T(2,128)} %broadcast_in_dim.23.refs_4_.refs_5_, ...), custom_call_target="tpu_custom_call" | custom-call | tf_op jit(solution)/shard_map/step0/pallas_call | solution.py:345
  93.7 0.8 convert_reduce_fusion.3
  94.5 0.7 fusion.3
  95.3 0.6 maximum_bitcast_fusion.refs_1_
  95.9 2.4 gather_fusion
  98.3 85.6 %step1.1 = (s32[32,128]{1,0:T(8,128)}, bf16[32,2304]{1,0:T(8,128)(2,1)}, f32[2,32,128]{2,1,0:T(8,128)}) custom-call(bf16[2,16,2304]{2,1,0:T(8,128)(2,1)} %bitcast.32, f32[2,2,16,128]{3,2,1,0:T(8,128)} %maximum_bitcast_fusion.refs_1_, bf16[1,2304]{1,0:T(2,128)(2,1)} %broadcast_in_dim.20.refs_1_.refs_2_, bf16[1,2304]{1,0:T(2,128)(2,1)} %broadcast_in_dim.21.refs_2_.refs_3_, ...), custom_call_target="tpu_custom_call" | custom-call | tf_op jit(solution)/shard_map/step1/pallas_call | solution.py:345
  183.9 1.4 slice_reduce_fusion.3
  185.3 0.8 convert_reduce_fusion.2
  186.1 0.7 fusion.2
  186.9 0.6 maximum_bitcast_fusion.1.refs_1_
  187.5 2.4 gather_fusion.1
  189.8 86.3 %step2.1 = (s32[32,128]{1,0:T(8,128)}, bf16[32,2304]{1,0:T(8,128)(2,1)}, f32[2,32,128]{2,1,0:T(8,128)}) custom-call(bf16[2,16,2304]{2,1,0:T(8,128)(2,1)} %bitcast.33, f32[2,2,16,128]{3,2,1,0:T(8,128)} %maximum_bitcast_fusion.1.refs_1_, bf16[1,2304]{1,0:T(2,128)(2,1)} %broadcast_in_dim.20.refs_1_.refs_2_, bf16[1,2304]{1,0:T(2,128)(2,1)} %broadcast_in_dim.21.refs_2_.refs_3_, ...), custom_call_target="tpu_custom_call" | custom-call | tf_op jit(solution)/shard_map/step2/pallas_call | solution.py:345
  276.2 0.0 copy-start
  276.2 0.8 slice_reduce_fusion.2
  277.0 0.8 convert_reduce_fusion.1
  277.8 0.7 fusion.1
  278.6 0.6 maximum_bitcast_fusion.2.refs_1_
  279.2 2.4 gather_fusion.2
  281.6 85.6 %step3.1 = (s32[32,128]{1,0:T(8,128)}, bf16[32,2304]{1,0:T(8,128)(2,1)}, f32[2,32,128]{2,1,0:T(8,128)}) custom-call(bf16[2,16,2304]{2,1,0:T(8,128)(2,1)} %bitcast.31, f32[2,2,16,128]{3,2,1,0:T(8,128)} %maximum_bitcast_fusion.2.refs_1_, bf16[1,2304]{1,0:T(2,128)(2,1)} %broadcast_in_dim.20.refs_1_.refs_2_, bf16[1,2304]{1,0:T(2,128)(2,1)} %broadcast_in_dim.21.refs_2_.refs_3_, ...), custom_call_target="tpu_custom_call" | custom-call | tf_op jit(solution)/shard_map/step3/pallas_call | solution.py:345
  367.2 0.8 slice_reduce_fusion.1
  368.0 0.8 convert_reduce_fusion
  368.8 0.7 fusion
  369.6 1.7 gather_fusion.3
  371.3 7.4 %step4.1 = (s32[32,128]{1,0:T(8,128)S(1)}, bf16[32,2304]{1,0:T(8,128)(2,1)S(1)}) custom-call(bf16[2,16,2304]{2,1,0:T(8,128)(2,1)S(1)} %bitcast.30, f32[2,2,16,128]{3,2,1,0:T(8,128)S(1)} %maximum_bitcast_fusion.3.refs_1_), custom_call_target="tpu_custom_call" | custom-call | tf_op jit(solution)/shard_map/step4/pallas_call | solution.py:345
  378.7 0.1 slice_reduce_fusion
  378.8 0.6 pad_add_fusion
  379.4 0.7 copy.18
  (6 shorter events, 0.0 us)
Async XLA Ops:
  276.2 102.6 %copy-start = (s32[32]{0:T(128)S(1)}, s32[32]{0:T(128)}, u32[]{:S(2)}) copy-start(s32[32]{0:T(128)} %slice_reduce_fusion.3) | copy-start | bytes 388

commit v2 on v1

--- a/solution.py
+++ b/solution.py
@@ -17,19 +17,30 @@
 NSUB = 5
 GROUP = SUB * NSUB
 RING_GROUPS = 4
-OWN = 5
+HEAD = 8
+TAIL = 1
+OWN = HEAD + TAIL
 NEG = -3.0e38
+
+
+def gain(ref):
+    return ref[...].astype(jnp.float32).reshape(1, ref.shape[0])
 
 
 def rms_scale(x_f32, gain_row):
     mean_sq = jnp.mean(x_f32 * x_f32, axis=-1, keepdims=True)
-    return x_f32 * lax.rsqrt(mean_sq + EPSILON) * (1.0 + gain_row.astype(jnp.float32))
+    return x_f32 * lax.rsqrt(mean_sq + EPSILON) * (1.0 + gain_row)
 
 
 def remote(src, dst, sem, peer):
     return pltpu.make_async_remote_copy(
         src_ref=src, dst_ref=dst, send_sem=sem.at[0], recv_sem=sem.at[1], device_id=peer, device_id_type=MESH
     )
+
+
+def as_line(wide):
+    eye = lax.broadcasted_iota(jnp.int32, wide.shape, 0) == lax.broadcasted_iota(jnp.int32, wide.shape, 1)
+    return jnp.sum(jnp.where(eye, wide, 0), axis=0, keepdims=True)
 
 
 def step_kernel(cfg, *refs):
@@ -40,12 +51,14 @@
         (hid_ref,) = take(1)
     else:
         rows_ref, meta_ref = take(2)
+        if last:
+            old_refs = take(step - 1)
     if not last:
         pre_ref, post_ref, fin_ref, temp_ref, wg_ref, wu_ref, wd_ref, emb_ref, noise_ref = take(9)
     if not first:
         tok_ref, hout_ref = take(2)
     if not last:
-        best_ref = take(1)[0]
+        best_ref, line_ref = take(2)
     if not first:
         rows_a, meta_a, rows_m, meta_m, rows_b, meta_b, rows_f, meta_f, rows_c, meta_c, sem_rows, sem_meta = take(12)
     if not last:
@@ -71,8 +84,12 @@
             pltpu.make_async_copy(wd_ref, ring.at[pl.ds(2 * width, inner)], sem_w.at[2]),
         ]
 
+        def group_of(i):
+            moved = jnp.where(i < HEAD + half, dp * half, half)
+            return i + jnp.where(i < HEAD, 0, moved)
+
         def e_copy(i, j):
-            group = i + jnp.where(i < OWN, 0, dp * half)
+            group = group_of(i)
             slot = lax.rem(i + 3, RING_GROUPS)
             return pltpu.make_async_copy(
                 emb_ref.at[pl.ds(group * GROUP + j * SUB, SUB)],
@@ -85,13 +102,13 @@
                 e_copy(i, j).start()
 
         def no_copy(i):
-            group = i + jnp.where(i < OWN, 0, dp * half)
+            group = group_of(i)
             return pltpu.make_async_copy(
                 noise_ref.at[step, :, pl.ds(group * GROUP, GROUP)], nz_own.at[i], sem_no.at[i]
             )
 
         def nr_copy(j):
-            group = OWN + (1 - dp) * half + j
+            group = HEAD + (1 - dp) * half + j
             return pltpu.make_async_remote_copy(
                 src_ref=noise_ref.at[step, :, pl.ds(group * GROUP, GROUP)],
                 dst_ref=nz_oth.at[j],
@@ -155,7 +172,12 @@
         r_f, r_c = rows_f[...].astype(jnp.float32), rows_c[...].astype(jnp.float32)
         t_f, t_c = meta_f[1], meta_c[1]
         picked = jnp.concatenate([jnp.where(low, r_f, r_c), jnp.where(low, r_c, r_f)], axis=0)
-        tok_ref[...] = jnp.concatenate([jnp.where(low, t_f, t_c), jnp.where(low, t_c, t_f)], axis=0).astype(jnp.int32)
+        token = jnp.concatenate([jnp.where(low, t_f, t_c), jnp.where(low, t_c, t_f)], axis=0).astype(jnp.int32)
+        if last:
+            for k, line in enumerate([ref[...] for ref in old_refs] + [as_line(token)]):
+                tok_ref[k : k + 1] = line[:, : token.shape[0]]
+        else:
+            tok_ref[...] = as_line(token)
         hid_bf = (picked * embed_scale).astype(jnp.bfloat16)
         hout_ref[...] = hid_bf
         hid = hid_bf.astype(jnp.float32)
@@ -166,7 +188,7 @@
     batch = hid.shape[0]
     quarter = batch // 4
     hid32[...] = hid.reshape(4, quarter, width)
-    normed = rms_scale(hid, pre_ref[...]).astype(jnp.bfloat16)
+    normed = rms_scale(hid, gain(pre_ref)).astype(jnp.bfloat16)
     f_two[pl.ds(0, batch)] = normed
     w_copies[0].wait()
     w_copies[1].wait()
@@ -202,9 +224,9 @@
     rb.wait()
     down_sum = half_s[chip] + part_b[...]
     place = 2 * core + chip
-    post_out = rms_scale(down_sum, post_ref[...]).astype(jnp.bfloat16)
+    post_out = rms_scale(down_sum, gain(post_ref)).astype(jnp.bfloat16)
     resid = (hid32[place] + post_out.astype(jnp.float32)).astype(jnp.bfloat16)
-    final_in = rms_scale(resid.astype(jnp.float32), fin_ref[...]).astype(jnp.bfloat16)
+    final_in = rms_scale(resid.astype(jnp.float32), gain(fin_ref)).astype(jnp.bfloat16)
     f_send[...] = final_in
     f_copies = [remote(f_send, f_all.at[k], sem_f.at[k], peer) for k, peer in enumerate((sib, over, diag))]
     for copy in f_copies:
@@ -230,12 +252,14 @@
 
     bv[...] = jnp.full_like(bv, NEG)
     bi[...] = jnp.zeros_like(bi)
-    c1 = temp_ref[0:1, 0:1]
-    c2 = temp_ref[1:2, 0:1]
+    heat = jnp.full((1, 128), temp_ref[0, 0], jnp.float32)
+    fold = jnp.where(heat > 2.0**64, 2.0**-64, 1.0)
+    c1 = (SOFT_CAP * fold)[:, :1]
+    c2 = (1.0 / (heat * fold))[:, :1]
 
     def score(i, rows, nz_refs):
         slot = lax.rem(i + 3, RING_GROUPS)
-        group = i + jnp.where(i < OWN, 0, dp * half)
+        group = group_of(i)
         for j in range(NSUB):
             e_copy(i, j).wait()
         lhs = f_two[pl.ds(0, rows)]
@@ -257,21 +281,19 @@
         def _():
             e_start(i + RING_GROUPS)
 
-    @pl.loop(0, OWN)
+    def own(i):
+        no_copy(i).wait()
+        score(i, batch, [nz_own.at[i]])
+
+    pl.loop(0, HEAD)(own)
+    fo.wait()
+    f_two[pl.ds(batch, batch)] = f_oth[...]
+
+    @pl.loop(HEAD, HEAD + half)
     def _(i):
         no_copy(i).wait()
-        score(i, batch, [nz_own.at[i]])
-
-    fo.wait()
-    f_two[pl.ds(batch, batch)] = f_oth[...]
-
-    @pl.loop(OWN, n_iter)
-    def _(i):
-        no_copy(i).wait()
-        nr_copy(i - OWN).wait_recv()
-        score(i, 2 * batch, [nz_own.at[i], nz_oth.at[i - OWN]])
-
-    pl.loop(0, half)(lambda j: nr_copy(j).wait_send())
+        nr_copy(i - HEAD).wait_recv()
+        score(i, 2 * batch, [nz_own.at[i], nz_oth.at[i - HEAD]])
 
     def settle(part):
         val = bv[pl.ds(part * batch, batch)]
@@ -286,11 +308,49 @@
     best_oth[1] = o_row
     by = remote(best_oth, best_in, sem_by, pair)
     by.start()
+    pl.loop(HEAD + half, n_iter)(own)
+    pl.loop(0, half)(lambda j: nr_copy(j).wait_send())
     m_val, m_row = settle(0)
     by.wait()
     keep = m_val >= best_in[0]
-    best_ref[0] = jnp.where(keep, m_val, best_in[0])
-    best_ref[1] = jnp.where(keep, m_row, best_in[1])
+    top = jnp.where(keep, m_val, best_in[0])
+    row = jnp.where(keep, m_row, best_in[1])
+    offset = (tp * (n_group * GROUP)).astype(jnp.float32)
+    hb = batch // 2
+    for part in range(2):
+        best_ref[part, 0] = top[part * hb : (part + 1) * hb]
+        best_ref[part, 1] = row[part * hb : (part + 1) * hb] + offset
+    line_ref[...] = as_line(row.astype(jnp.int32))
+
+
+def lookup_kernel(line_ref, emb_ref, out_ref, tiles, sem):
+    half, batch = out_ref.shape[1], 2 * out_ref.shape[1]
+    for r in range(batch):
+        base = pl.multiple_of(lax.div(line_ref[0, r], 8) * 8, 8)
+        pltpu.make_async_copy(emb_ref.at[pl.ds(base, 8)], tiles.at[pl.ds(8 * r, 8)], sem).start()
+    shape = (batch, 8 * batch)
+    place = lax.broadcasted_iota(jnp.int32, (batch, 1), 0)
+    want = 8 * place
+    for r in range(batch):
+        want = want + jnp.where(place == r, lax.rem(line_ref[0, r], 8), 0)
+    pick = (lax.broadcasted_iota(jnp.int32, shape, 1) == want).astype(jnp.bfloat16)
+    pltpu.make_async_copy(emb_ref.at[pl.ds(0, 8 * batch)], tiles, sem).wait()
+    rows = jnp.dot(pick, tiles[...], preferred_element_type=jnp.float32).astype(jnp.bfloat16)
+    out_ref[0] = rows[:half]
+    out_ref[1] = rows[half:]
+
+
+def lookup(line, batch, embedding):
+    width = embedding.shape[1]
+    return pl.pallas_call(
+        lookup_kernel,
+        out_shape=jax.ShapeDtypeStruct((2, batch // 2, width), jnp.bfloat16),
+        in_specs=[pl.BlockSpec(memory_space=pltpu.SMEM), pl.BlockSpec(memory_space=pl.ANY)],
+        out_specs=pl.BlockSpec(memory_space=pltpu.VMEM),
+        scratch_shapes=[pltpu.VMEM((8 * batch, width), jnp.bfloat16), pltpu.SemaphoreType.DMA(())],
+        compiler_params=pltpu.CompilerParams(vmem_limit_bytes=66_000_000),
+        name="lookup",
+    )(line, embedding)
 
 
 def call_step(step, steps, batch, width, inner, vocab_local, embed_scale, operands):
@@ -302,16 +362,19 @@
     half = (n_group - OWN) // 2
     n_iter = OWN + half
     hb, quarter = batch // 2, batch // 4
-    in_specs = [vmem] * (1 if first else 2)
-    if not last:
-        in_specs += [vmem] * 4 + [hbm] * 5
+    in_specs = [vmem] * (1 if first else 2 + (step - 1) * last)
+    if not last:
+        in_specs += [vmem] * 3 + [pl.BlockSpec(memory_space=pltpu.SMEM)] + [hbm] * 5
     outs, scratch = [], []
     if not first:
-        outs += [jax.ShapeDtypeStruct((batch, 128), i32), jax.ShapeDtypeStruct((batch, width), bf16)]
+        outs += [jax.ShapeDtypeStruct((steps, batch) if last else (1, 128), i32), jax.ShapeDtypeStruct((batch, width), bf16)]
         rows, meta = pltpu.VMEM((hb, width), bf16), pltpu.VMEM((2, hb, 128), f32)
         scratch += [rows, meta] * 5 + [dma((3, 2)), dma((3, 2))]
     if not last:
-        outs += [jax.ShapeDtypeStruct((2, batch, 128), f32)]
+        outs += [
+            jax.ShapeDtypeStruct((2, 2, hb, 128), f32),
+            jax.ShapeDtypeStruct((1, 128), i32),
+        ]
         scratch += [
             pltpu.VMEM((RING_GROUPS * GROUP, width), bf16),
             pltpu.VMEM((n_iter, batch, GROUP), f32),
@@ -349,7 +412,7 @@
         out_specs=[vmem] * len(outs),
         scratch_shapes=scratch,
         compiler_params=pltpu.CompilerParams(
-            collective_id=step, has_side_effects=True, vmem_limit_bytes=66_000_000 if not last else 16_000_000
+            collective_id=step, has_side_effects=True, vmem_limit_bytes=66_000_000
         ),
         name=f"step{step}",
     )(*operands)
@@ -360,25 +423,17 @@
         vocab_local, width = embedding.shape
         batch, steps = start_hidden.shape[0], step_noise.shape[0]
         inner = w_gate.shape[1]
-        row_offset = (lax.axis_index("tp") * vocab_local).astype(jnp.float32)
         embed_scale = float(np.float64(math.sqrt(width)).astype(jnp.bfloat16))
-        a = jnp.where(temperature > 2.0**64, 2.0**-64, 1.0).astype(jnp.float32)
-        temp = jnp.broadcast_to(jnp.stack([SOFT_CAP * a, 1.0 / (temperature * a)])[:, None], (2, 128))
-        norms = [v[None] for v in (pre_norm, post_norm, final_norm)]
-        common = [*norms, temp, w_gate, w_up, w_down, embedding, step_noise]
+        common = [pre_norm, post_norm, final_norm, temperature.reshape(1, 1), w_gate, w_up, w_down, embedding, step_noise]
         sizes = (steps, batch, width, inner, vocab_local, embed_scale)
-        (best,) = call_step(0, *sizes, [start_hidden, *common])
-        token_list = []
-        for step in range(1, steps + 1):
-            local_row = best[1, :, 0].astype(jnp.int32)
-            rows = jnp.take(embedding, local_row, axis=0, mode="clip").reshape(2, batch // 2, width)
-            meta = jnp.stack([best[0], best[1] + row_offset]).reshape(2, 2, batch // 2, 128).transpose(1, 0, 2, 3)
-            outs = call_step(step, *sizes, [rows, meta, *(common if step < steps else [])])
-            token_list.append(outs[0][:, 0])
-            hidden = outs[1]
-            if step < steps:
-                best = outs[2]
-        return jnp.stack(token_list), hidden
+        best, line = call_step(0, *sizes, [start_hidden, *common])
+        lines = []
+        for step in range(1, steps):
+            outs = call_step(step, *sizes, [lookup(line, batch, embedding), best, *common])
+            lines.append(outs[0])
+            best, line = outs[2:]
+        tokens, hidden = call_step(steps, *sizes, [lookup(line, batch, embedding), best, *lines])
+        return tokens, hidden
 
     return jax.shard_map(
         local_steps,

time: 382 us -> 373 us (0.976)
  Pallas kernels: 353 us -> 368 us
  local copies, waits for them, and re-layouts: 17.1 us -> 2.82 us
  other arithmetic: 8.83 us -> 0 us
    pallas_call x0 -> x4, Pallas kernels: none -> 11.6 us  [lookup(): pl.pallas_call(lookup_kernel, out_shape=jax.ShapeDtypeStruct((2, batch //...]
    gather x4 -> x0, local copies, waits for them, and re-layouts: 8.83 us -> none  [local_steps(): jnp.take(embedding, local_row, axis=0, mode='clip')]
    broadcast_in_dim x4 -> x0, local copies, waits for them, and re-layouts: 4.51 us -> none  [the longest x3 3.88 us: local_steps(): norms = [v[None] for v in (pre_norm, post_norm, final_norm)]]
where the time goes in v2:
time: 373 us; the launch traced here: 372 us
  Pallas kernels  368 us (99%)
    pallas_call x5, Pallas kernels, call_step(): pl.pallas_call(functools.partial(step_kernel, (step, first, last, n_group...  356 us
    pallas_call x4, Pallas kernels, lookup(): pl.pallas_call(lookup_kernel, out_shape=jax.ShapeDtypeStruct((2, batch //...  11.6 us

profile of v2, /device:TPU:0, one launch (start us, length us, event | category | flops | bytes accessed | tf_op | source)
XLA Modules:
  0.0 372.1 jit_solution(2610963160713977770)
XLA Ops:
  1.3 87.0 %step0.1 = (f32[2,2,16,128]{3,2,1,0:T(8,128)}, s32[1,128]{1,0:T(1,128)}) custom-call(bf16[32,2304]{1,0:T(8,128)(2,1)} %refs_0_.1, bf16[2304]{0:T(1024)(128)(2,1)} %refs_2_.7, bf16[2304]{0:T(1024)(128)(2,1)} %refs_3_.7, bf16[2304]{0:T(1024)(128)(2,1)} %refs_4_.5, f32[1,1]{1,0:T(1,128)} %bitcast.1.refs_4_, bf16[2304,2304]{1,0:T(8,128)(2,1)} %refs_6_.7, ...), custom_call_target="tpu_custom_call" | custom-call | tf_op jit(solution)/shard_map/step0/pallas_call | solution.py:408
  88.3 2.9 lookup.4.refs_0_
  91.2 87.5 %step1.1 = (s32[1,128]{1,0:T(1,128)}, bf16[32,2304]{1,0:T(8,128)(2,1)}, f32[2,2,16,128]{3,2,1,0:T(8,128)}, s32[1,128]{1,0:T(1,128)}) custom-call(bf16[2,16,2304]{2,1,0:T(8,128)(2,1)} %lookup.4.refs_0_, f32[2,2,16,128]{3,2,1,0:T(8,128)} %get-tuple-element.14.refs_1_, bf16[2304]{0:T(1024)(128)(2,1)} %refs_2_.7, bf16[2304]{0:T(1024)(128)(2,1)} %refs_3_.7, ...), custom_call_target="tpu_custom_call" | custom-call | tf_op jit(solution)/shard_map/step1/pallas_call | solution.py:408
  178.8 2.9 lookup.5.refs_0_
  181.7 86.3 %step2.1 = (s32[1,128]{1,0:T(1,128)}, bf16[32,2304]{1,0:T(8,128)(2,1)}, f32[2,2,16,128]{3,2,1,0:T(8,128)}, s32[1,128]{1,0:T(1,128)}) custom-call(bf16[2,16,2304]{2,1,0:T(8,128)(2,1)} %lookup.5.refs_0_, f32[2,2,16,128]{3,2,1,0:T(8,128)} %get-tuple-element.16.refs_1_, bf16[2304]{0:T(1024)(128)(2,1)} %refs_2_.7, bf16[2304]{0:T(1024)(128)(2,1)} %refs_3_.7, ...), custom_call_target="tpu_custom_call" | custom-call | tf_op jit(solution)/shard_map/step2/pallas_call | solution.py:408
  268.0 2.9 lookup.6.refs_0_
  270.9 86.5 %step3.1 = (s32[1,128]{1,0:T(1,128)}, bf16[32,2304]{1,0:T(8,128)(2,1)}, f32[2,2,16,128]{3,2,1,0:T(8,128)}, s32[1,128]{1,0:T(1,128)}) custom-call(bf16[2,16,2304]{2,1,0:T(8,128)(2,1)} %lookup.6.refs_0_, f32[2,2,16,128]{3,2,1,0:T(8,128)} %get-tuple-element.18.refs_1_, bf16[2304]{0:T(1024)(128)(2,1)} %refs_2_.7, bf16[2304]{0:T(1024)(128)(2,1)} %refs_3_.7, ...), custom_call_target="tpu_custom_call" | custom-call | tf_op jit(solution)/shard_map/step3/pallas_call | solution.py:408
  357.4 2.9 lookup.7.refs_0_
  360.3 8.9 %step4.1 = (s32[4,32]{1,0:T(4,128)}, bf16[32,2304]{1,0:T(8,128)(2,1)}) custom-call(bf16[2,16,2304]{2,1,0:T(8,128)(2,1)} %lookup.7.refs_0_, f32[2,2,16,128]{3,2,1,0:T(8,128)} %get-tuple-element.20.refs_1_, s32[1,128]{1,0:T(1,128)} %get-tuple-element.21.refs_2_, s32[1,128]{1,0:T(1,128)} %get-tuple-element.22.refs_3_, s32[1,128]{1,0:T(1,128)} %get-tuple-element.23.refs_4_), custom_call_target="tpu_custom_call" | custom-call | tf_op jit(solution)/shard_map/step4/pallas_call | solution.py:408
  369.3 1.2 copy.15
  370.5 1.6 copy.16

commit v3 on v2

--- a/solution.py
+++ b/solution.py
@@ -17,7 +17,8 @@
 NSUB = 5
 GROUP = SUB * NSUB
 RING_GROUPS = 4
-HEAD = 8
+TURNED = (1, 2, 4)
+HEAD = 6
 TAIL = 1
 OWN = HEAD + TAIL
 NEG = -3.0e38
@@ -63,8 +64,8 @@
         rows_a, meta_a, rows_m, meta_m, rows_b, meta_b, rows_f, meta_f, rows_c, meta_c, sem_rows, sem_meta = take(12)
     if not last:
         (ring, nz_own, nz_oth, part_s, part_a, half_s, part_b, f_send, f_all, f_own, f_oth, f_two,
-         hid32, gate_s, bv, bi, best_oth, best_in,
-         sem_w, sem_e, sem_no, sem_ns, sem_nr, sem_ra, sem_rb, sem_f, sem_fo, sem_by) = take(28)
+         hid32, gate_s, turned, bv, bi, best_oth, best_in,
+         sem_w, sem_e, sem_no, sem_ns, sem_nr, sem_ra, sem_rb, sem_f, sem_fo, sem_by) = take(29)
 
     dp, tp = lax.axis_index("dp"), lax.axis_index("tp")
     core, chip = lax.rem(tp, 2), lax.div(tp, 2)
@@ -118,10 +119,8 @@
                 device_id_type=MESH,
             )
 
-        for copy in w_copies:
-            copy.start()
-        e_start(0)
-        pl.loop(0, n_iter)(lambda i: no_copy(i).start())
+        w_copies[0].start()
+        w_copies[1].start()
 
     barrier = pltpu.get_barrier_semaphore()
     peers = (sib, over) if last else (sib, over, diag, pair)
@@ -129,12 +128,19 @@
         pl.semaphore_signal(barrier, inc=1, device_id=peer, device_id_type=MESH)
     pl.semaphore_wait(barrier, len(peers))
 
+    def fetch_head():
+        e_start(0)
+        pl.loop(0, n_iter)(lambda i: no_copy(i).start())
+
     if not last:
         early = 3
         pl.loop(0, early)(lambda j: nr_copy(j).start())
 
     if first:
         hid = hid_ref[...].astype(jnp.float32)
+        w_copies[2].start()
+        w_copies[0].wait()
+        fetch_head()
     else:
         a_rows = remote(rows_ref.at[1 - core], rows_a, sem_rows.at[0], sib)
         a_meta = remote(meta_ref.at[1 - core], meta_a, sem_meta.at[0], sib)
@@ -142,6 +148,8 @@
         a_meta.start()
         a_rows.wait()
         a_meta.wait()
+        if not last:
+            w_copies[2].start()
         mine = meta_ref[core]
         seen = meta_a[...]
         keep = mine[0] >= seen[0]
@@ -168,6 +176,9 @@
         c_meta.start()
         c_rows.wait()
         c_meta.wait()
+        if not last:
+            w_copies[0].wait()
+            fetch_head()
         low = core == 0
         r_f, r_c = rows_f[...].astype(jnp.float32), rows_c[...].astype(jnp.float32)
         t_f, t_c = meta_f[1], meta_c[1]
@@ -190,7 +201,6 @@
     hid32[...] = hid.reshape(4, quarter, width)
     normed = rms_scale(hid, gain(pre_ref)).astype(jnp.bfloat16)
     f_two[pl.ds(0, batch)] = normed
-    w_copies[0].wait()
     w_copies[1].wait()
     col = 768
 
@@ -265,7 +275,13 @@
         lhs = f_two[pl.ds(0, rows)]
         for j in range(NSUB):
             block = ring[pl.ds(pl.multiple_of(slot * GROUP + j * SUB, SUB), SUB), :]
-            z = lax.dot_general(lhs, block, (((1,), (1,)), ((), ())), preferred_element_type=jnp.float32)
+            if j in TURNED:
+                spare = TURNED.index(j) % turned.shape[0]
+                for k in range(0, width, 256):
+                    turned[spare, pl.ds(k, 256)] = block[:, k : k + 256].T
+                z = jnp.dot(lhs, turned[spare], preferred_element_type=jnp.float32)
+            else:
+                z = lax.dot_general(lhs, block, (((1,), (1,)), ((), ())), preferred_element_type=jnp.float32)
             s = jnp.tanh(z * (1.0 / SOFT_CAP)) * c1 * c2
             for part, nz in enumerate(nz_refs):
                 take_rows = pl.ds(part * batch, batch)
@@ -285,12 +301,7 @@
         no_copy(i).wait()
         score(i, batch, [nz_own.at[i]])
 
-    pl.loop(0, HEAD)(own)
-    fo.wait()
-    f_two[pl.ds(batch, batch)] = f_oth[...]
-
-    @pl.loop(HEAD, HEAD + half)
-    def _(i):
+    def shared(i):
         no_copy(i).wait()
         nr_copy(i - HEAD).wait_recv()
         score(i, 2 * batch, [nz_own.at[i], nz_oth.at[i - HEAD]])
@@ -303,12 +314,22 @@
         row = jnp.min(jnp.where(val == top, ids, 3.0e7), axis=1, keepdims=True)
         return jnp.broadcast_to(top, (batch, 128)), jnp.broadcast_to(row, (batch, 128))
 
-    o_val, o_row = settle(1)
-    best_oth[0] = o_val
-    best_oth[1] = o_row
     by = remote(best_oth, best_in, sem_by, pair)
-    by.start()
-    pl.loop(HEAD + half, n_iter)(own)
+
+    @pl.loop(0, 2)
+    def _(phase):
+        pl.loop(jnp.where(phase == 0, 0, HEAD + half), jnp.where(phase == 0, HEAD, n_iter))(own)
+
+        @pl.when(phase == 0)
+        def _():
+            fo.wait()
+            f_two[pl.ds(batch, batch)] = f_oth[...]
+            pl.loop(HEAD, HEAD + half)(shared)
+            o_val, o_row = settle(1)
+            best_oth[0] = o_val
+            best_oth[1] = o_row
+            by.start()
+
     pl.loop(0, half)(lambda j: nr_copy(j).wait_send())
     m_val, m_row = settle(0)
     by.wait()
@@ -390,6 +411,7 @@
             pltpu.VMEM((2 * batch, width), bf16),
             pltpu.VMEM((4, quarter, width), f32),
             pltpu.VMEM((batch, inner), bf16),
+            pltpu.VMEM((2, width, SUB), bf16),
             pltpu.VMEM((2 * batch, 256), f32),
             pltpu.VMEM((2 * batch, 256), i32),
             pltpu.VMEM((2, batch, 128), f32),

time: 373 us -> 338 us (0.906)
  Pallas kernels: 368 us -> 333 us
    pallas_call x5, Pallas kernels: 356 us -> 322 us  [call_step(): pl.pallas_call(functools.partial(step_kernel, (step, first, last, n_group...]
where the time goes in v3:
time: 338 us
  Pallas kernels  333 us (99%)
    pallas_call x5, Pallas kernels, call_step(): pl.pallas_call(functools.partial(step_kernel, (step, first, last, n_group...  322 us
    pallas_call x4, Pallas kernels, lookup(): pl.pallas_call(lookup_kernel, out_shape=jax.ShapeDtypeStruct((2, batch //...  11.6 us

profile of v3, /device:TPU:0, one launch (start us, length us, event | category | flops | bytes accessed | tf_op | source)
XLA Modules:
  0.0 337.6 jit_solution(800660979587066744)
XLA Ops:
  1.3 80.0 %step0.1 = (f32[2,2,16,128]{3,2,1,0:T(8,128)}, s32[1,128]{1,0:T(1,128)}) custom-call(bf16[32,2304]{1,0:T(8,128)(2,1)} %refs_0_.1, bf16[2304]{0:T(1024)(128)(2,1)} %refs_2_.7, bf16[2304]{0:T(1024)(128)(2,1)} %refs_3_.7, bf16[2304]{0:T(1024)(128)(2,1)} %refs_4_.5, f32[1,1]{1,0:T(1,128)} %bitcast.1.refs_4_, bf16[2304,2304]{1,0:T(8,128)(2,1)} %refs_6_.7, ...), custom_call_target="tpu_custom_call" | custom-call | tf_op jit(solution)/shard_map/step0/pallas_call | solution.py:430
  81.3 2.9 lookup.4.refs_0_
  84.2 77.5 %step1.1 = (s32[1,128]{1,0:T(1,128)}, bf16[32,2304]{1,0:T(8,128)(2,1)}, f32[2,2,16,128]{3,2,1,0:T(8,128)}, s32[1,128]{1,0:T(1,128)}) custom-call(bf16[2,16,2304]{2,1,0:T(8,128)(2,1)} %lookup.4.refs_0_, f32[2,2,16,128]{3,2,1,0:T(8,128)} %get-tuple-element.14.refs_1_, bf16[2304]{0:T(1024)(128)(2,1)} %refs_2_.7, bf16[2304]{0:T(1024)(128)(2,1)} %refs_3_.7, ...), custom_call_target="tpu_custom_call" | custom-call | tf_op jit(solution)/shard_map/step1/pallas_call | solution.py:430
  161.8 2.9 lookup.5.refs_0_
  164.7 77.6 %step2.1 = (s32[1,128]{1,0:T(1,128)}, bf16[32,2304]{1,0:T(8,128)(2,1)}, f32[2,2,16,128]{3,2,1,0:T(8,128)}, s32[1,128]{1,0:T(1,128)}) custom-call(bf16[2,16,2304]{2,1,0:T(8,128)(2,1)} %lookup.5.refs_0_, f32[2,2,16,128]{3,2,1,0:T(8,128)} %get-tuple-element.16.refs_1_, bf16[2304]{0:T(1024)(128)(2,1)} %refs_2_.7, bf16[2304]{0:T(1024)(128)(2,1)} %refs_3_.7, ...), custom_call_target="tpu_custom_call" | custom-call | tf_op jit(solution)/shard_map/step2/pallas_call | solution.py:430
  242.2 2.9 lookup.6.refs_0_
  245.1 77.7 %step3.1 = (s32[1,128]{1,0:T(1,128)}, bf16[32,2304]{1,0:T(8,128)(2,1)}, f32[2,2,16,128]{3,2,1,0:T(8,128)}, s32[1,128]{1,0:T(1,128)}) custom-call(bf16[2,16,2304]{2,1,0:T(8,128)(2,1)} %lookup.6.refs_0_, f32[2,2,16,128]{3,2,1,0:T(8,128)} %get-tuple-element.18.refs_1_, bf16[2304]{0:T(1024)(128)(2,1)} %refs_2_.7, bf16[2304]{0:T(1024)(128)(2,1)} %refs_3_.7, ...), custom_call_target="tpu_custom_call" | custom-call | tf_op jit(solution)/shard_map/step3/pallas_call | solution.py:430
  322.9 2.9 lookup.7.refs_0_
  325.8 8.9 %step4.1 = (s32[4,32]{1,0:T(4,128)}, bf16[32,2304]{1,0:T(8,128)(2,1)}) custom-call(bf16[2,16,2304]{2,1,0:T(8,128)(2,1)} %lookup.7.refs_0_, f32[2,2,16,128]{3,2,1,0:T(8,128)} %get-tuple-element.20.refs_1_, s32[1,128]{1,0:T(1,128)} %get-tuple-element.21.refs_2_, s32[1,128]{1,0:T(1,128)} %get-tuple-element.22.refs_3_, s32[1,128]{1,0:T(1,128)} %get-tuple-element.23.refs_4_), custom_call_target="tpu_custom_call" | custom-call | tf_op jit(solution)/shard_map/step4/pallas_call | solution.py:430
  334.7 1.2 copy.15
  336.0 1.6 copy.16

commit v4 on v3

--- a/solution.py
+++ b/solution.py
@@ -13,13 +13,14 @@
 EPSILON = 1e-6
 MESH = pl.DeviceIdType.MESH
 
-SUB = 512
-NSUB = 5
+SUB = 640
+NSUB = 2
 GROUP = SUB * NSUB
-RING_GROUPS = 4
-TURNED = (1, 2, 4)
-HEAD = 6
-TAIL = 1
+RING_GROUPS = 8
+WEIGHT_GROUPS = 6
+CUTS = ((0, 512, False), (512, 768, True))
+HEAD = 14
+TAIL = 2
 OWN = HEAD + TAIL
 NEG = -3.0e38
 
@@ -63,9 +64,9 @@
     if not first:
         rows_a, meta_a, rows_m, meta_m, rows_b, meta_b, rows_f, meta_f, rows_c, meta_c, sem_rows, sem_meta = take(12)
     if not last:
-        (ring, nz_own, nz_oth, part_s, part_a, half_s, part_b, f_send, f_all, f_own, f_oth, f_two,
+        (ring, nz_own, nz_oth, part_s, part_a, half_s, part_b, f_send, f_all, f_pair, g_all, f_two,
          hid32, gate_s, turned, bv, bi, best_oth, best_in,
-         sem_w, sem_e, sem_no, sem_ns, sem_nr, sem_ra, sem_rb, sem_f, sem_fo, sem_by) = take(29)
+         sem_w, sem_e, sem_no, sem_ns, sem_nr, sem_ra, sem_rb, sem_f, sem_fo, sem_g, sem_by) = take(30)
 
     dp, tp = lax.axis_index("dp"), lax.axis_index("tp")
     core, chip = lax.rem(tp, 2), lax.div(tp, 2)
@@ -91,7 +92,7 @@
 
         def e_copy(i, j):
             group = group_of(i)
-            slot = lax.rem(i + 3, RING_GROUPS)
+            slot = lax.rem(i + WEIGHT_GROUPS, RING_GROUPS)
             return pltpu.make_async_copy(
                 emb_ref.at[pl.ds(group * GROUP + j * SUB, SUB)],
                 ring.at[pl.ds(slot * GROUP + j * SUB, SUB)],
@@ -130,10 +131,11 @@
 
     def fetch_head():
         e_start(0)
+        e_start(1)
         pl.loop(0, n_iter)(lambda i: no_copy(i).start())
 
     if not last:
-        early = 3
+        early = 6
         pl.loop(0, early)(lambda j: nr_copy(j).start())
 
     if first:
@@ -212,7 +214,8 @@
         up = jnp.dot(lhs, ring[pl.ds(width, width), cols], preferred_element_type=jnp.float32)
         gate_s[:, cols] = (jax.nn.gelu(gate, approximate=True) * up).astype(jnp.bfloat16)
 
-    e_start(1)
+    for i in range(2, 2 + (2 * width) // GROUP):
+        e_start(i)
     w_copies[2].wait()
 
     @pl.loop(0, width // col)
@@ -222,8 +225,8 @@
             gate_s[...], ring[pl.ds(2 * width, inner), cols], preferred_element_type=jnp.float32
         ).reshape(4, quarter, col)
 
-    e_start(2)
-    e_start(3)
+    for i in range(2 + (2 * width) // GROUP, RING_GROUPS):
+        e_start(i)
 
     ra = remote(part_s.at[pl.ds(2 * (1 - core), 2)], part_a, sem_ra, sib)
     ra.start()
@@ -239,26 +242,31 @@
     final_in = rms_scale(resid.astype(jnp.float32), gain(fin_ref)).astype(jnp.bfloat16)
     f_send[...] = final_in
     f_copies = [remote(f_send, f_all.at[k], sem_f.at[k], peer) for k, peer in enumerate((sib, over, diag))]
-    for copy in f_copies:
+    f_pair_copy = remote(f_send, f_pair, sem_fo, pair)
+    for copy in [*f_copies, f_pair_copy]:
         copy.start()
+    pl.loop(early, half)(lambda j: nr_copy(j).start())
     for copy in f_copies:
         copy.wait()
-    me_f, sib_f, over_f, diag_f = (v.astype(jnp.float32) for v in (f_send[...], f_all[0], f_all[1], f_all[2]))
     low_core, low_chip = core == 0, chip == 0
-    core0 = [jnp.where(low_core, a, b) for a, b in ((me_f, sib_f), (over_f, diag_f))]
-    core1 = [jnp.where(low_core, b, a) for a, b in ((me_f, sib_f), (over_f, diag_f))]
-    order = [
-        jnp.where(low_chip, core0[0], core0[1]),
-        jnp.where(low_chip, core0[1], core0[0]),
-        jnp.where(low_chip, core1[0], core1[1]),
-        jnp.where(low_chip, core1[1], core1[0]),
-    ]
-    f_bf = jnp.concatenate(order, axis=0).astype(jnp.bfloat16)
-    f_own[...] = f_bf
-    f_two[pl.ds(0, batch)] = f_bf
-    fo = remote(f_own, f_oth, sem_fo, pair)
-    fo.start()
-    pl.loop(early, half)(lambda j: nr_copy(j).start())
+
+    def in_order(mine_ref, others_ref):
+        me_f, sib_f, over_f, diag_f = (v.astype(jnp.float32) for v in (mine_ref[...], *(others_ref[k] for k in range(3))))
+        core0 = [jnp.where(low_core, a, b) for a, b in ((me_f, sib_f), (over_f, diag_f))]
+        core1 = [jnp.where(low_core, b, a) for a, b in ((me_f, sib_f), (over_f, diag_f))]
+        order = [
+            jnp.where(low_chip, core0[0], core0[1]),
+            jnp.where(low_chip, core0[1], core0[0]),
+            jnp.where(low_chip, core1[0], core1[1]),
+            jnp.where(low_chip, core1[1], core1[0]),
+        ]
+        return jnp.concatenate(order, axis=0).astype(jnp.bfloat16)
+
+    f_two[pl.ds(0, batch)] = in_order(f_send, f_all)
+    f_pair_copy.wait()
+    g_copies = [remote(f_pair, g_all.at[k], sem_g.at[k], peer) for k, peer in enumerate((sib, over, diag))]
+    for copy in g_copies:
+        copy.start()
 
     bv[...] = jnp.full_like(bv, NEG)
     bi[...] = jnp.zeros_like(bi)
@@ -268,30 +276,29 @@
     c2 = (1.0 / (heat * fold))[:, :1]
 
     def score(i, rows, nz_refs):
-        slot = lax.rem(i + 3, RING_GROUPS)
+        slot = lax.rem(i + WEIGHT_GROUPS, RING_GROUPS)
         group = group_of(i)
         for j in range(NSUB):
             e_copy(i, j).wait()
         lhs = f_two[pl.ds(0, rows)]
-        for j in range(NSUB):
-            block = ring[pl.ds(pl.multiple_of(slot * GROUP + j * SUB, SUB), SUB), :]
-            if j in TURNED:
-                spare = TURNED.index(j) % turned.shape[0]
+        for start, size, turn in CUTS:
+            block = ring[pl.ds(pl.multiple_of(slot * GROUP + start, 256), size), :]
+            if turn:
                 for k in range(0, width, 256):
-                    turned[spare, pl.ds(k, 256)] = block[:, k : k + 256].T
-                z = jnp.dot(lhs, turned[spare], preferred_element_type=jnp.float32)
+                    turned[pl.ds(k, 256)] = block[:, k : k + 256].T
+                z = jnp.dot(lhs, turned[...], preferred_element_type=jnp.float32)
             else:
                 z = lax.dot_general(lhs, block, (((1,), (1,)), ((), ())), preferred_element_type=jnp.float32)
             s = jnp.tanh(z * (1.0 / SOFT_CAP)) * c1 * c2
             for part, nz in enumerate(nz_refs):
                 take_rows = pl.ds(part * batch, batch)
-                for q in range(SUB // 256):
+                for q in range(size // 256):
                     v = s[part * batch : (part + 1) * batch, q * 256 : (q + 1) * 256]
-                    v = v + nz[:, j * SUB + q * 256 : j * SUB + (q + 1) * 256]
+                    v = v + nz[:, start + q * 256 : start + (q + 1) * 256]
                     old = bv[take_rows]
                     better = v > old
                     bv[take_rows] = jnp.where(better, v, old)
-                    bi[take_rows] = jnp.where(better, group * (GROUP // 256) + (j * (SUB // 256) + q), bi[take_rows])
+                    bi[take_rows] = jnp.where(better, group * (GROUP // 256) + (start // 256 + q), bi[take_rows])
 
         @pl.when(i + RING_GROUPS < n_iter)
         def _():
@@ -322,8 +329,9 @@
 
         @pl.when(phase == 0)
         def _():
-            fo.wait()
-            f_two[pl.ds(batch, batch)] = f_oth[...]
+            for copy in g_copies:
+                copy.wait()
+            f_two[pl.ds(batch, batch)] = in_order(f_pair, g_all)
             pl.loop(HEAD, HEAD + half)(shared)
             o_val, o_row = settle(1)
             best_oth[0] = o_val
@@ -406,12 +414,12 @@
             pltpu.VMEM((quarter, width), f32),
             pltpu.VMEM((quarter, width), bf16),
             pltpu.VMEM((3, quarter, width), bf16),
-            pltpu.VMEM((batch, width), bf16),
-            pltpu.VMEM((batch, width), bf16),
+            pltpu.VMEM((quarter, width), bf16),
+            pltpu.VMEM((3, quarter, width), bf16),
             pltpu.VMEM((2 * batch, width), bf16),
             pltpu.VMEM((4, quarter, width), f32),
             pltpu.VMEM((batch, inner), bf16),
-            pltpu.VMEM((2, width, SUB), bf16),
+            pltpu.VMEM((width, max(c[1] for c in CUTS if c[2])), bf16),
             pltpu.VMEM((2 * batch, 256), f32),
             pltpu.VMEM((2 * batch, 256), i32),
             pltpu.VMEM((2, batch, 128), f32),
@@ -425,6 +433,7 @@
             dma((2,)),
             dma((3, 2)),
             dma((2,)),
+            dma((3, 2)),
             dma((2,)),
         ]
     return pl.pallas_call(

time: 338 us -> 339 us (level)
  no operation moved by 1% of the time
where the time goes in v4:
time: 339 us
  Pallas kernels  334 us (99%)
    pallas_call x5, Pallas kernels, call_step(): pl.pallas_call(functools.partial(step_kernel, (step, first, last, n_group...  323 us
    pallas_call x4, Pallas kernels, lookup(): pl.pallas_call(lookup_kernel, out_shape=jax.ShapeDtypeStruct((2, batch //...  11.6 us

profile of v4, /device:TPU:0, one launch (start us, length us, event | category | flops | bytes accessed | tf_op | source)
XLA Modules:
  0.0 338.6 jit_solution(6759686113355970664)
XLA Ops:
  1.3 79.5 %step0.1 = (f32[2,2,16,128]{3,2,1,0:T(8,128)}, s32[1,128]{1,0:T(1,128)}) custom-call(bf16[32,2304]{1,0:T(8,128)(2,1)} %refs_0_.1, bf16[2304]{0:T(1024)(128)(2,1)} %refs_2_.7, bf16[2304]{0:T(1024)(128)(2,1)} %refs_3_.7, bf16[2304]{0:T(1024)(128)(2,1)} %refs_4_.5, f32[1,1]{1,0:T(1,128)} %bitcast.1.refs_4_, bf16[2304,2304]{1,0:T(8,128)(2,1)} %refs_6_.7, ...), custom_call_target="tpu_custom_call" | custom-call | tf_op jit(solution)/shard_map/step0/pallas_call | solution.py:439
  80.8 2.9 lookup.4.refs_0_
  83.7 78.1 %step1.1 = (s32[1,128]{1,0:T(1,128)}, bf16[32,2304]{1,0:T(8,128)(2,1)}, f32[2,2,16,128]{3,2,1,0:T(8,128)}, s32[1,128]{1,0:T(1,128)}) custom-call(bf16[2,16,2304]{2,1,0:T(8,128)(2,1)} %lookup.4.refs_0_, f32[2,2,16,128]{3,2,1,0:T(8,128)} %get-tuple-element.14.refs_1_, bf16[2304]{0:T(1024)(128)(2,1)} %refs_2_.7, bf16[2304]{0:T(1024)(128)(2,1)} %refs_3_.7, ...), custom_call_target="tpu_custom_call" | custom-call | tf_op jit(solution)/shard_map/step1/pallas_call | solution.py:439
  161.8 2.9 lookup.5.refs_0_
  164.7 78.2 %step2.1 = (s32[1,128]{1,0:T(1,128)}, bf16[32,2304]{1,0:T(8,128)(2,1)}, f32[2,2,16,128]{3,2,1,0:T(8,128)}, s32[1,128]{1,0:T(1,128)}) custom-call(bf16[2,16,2304]{2,1,0:T(8,128)(2,1)} %lookup.5.refs_0_, f32[2,2,16,128]{3,2,1,0:T(8,128)} %get-tuple-element.16.refs_1_, bf16[2304]{0:T(1024)(128)(2,1)} %refs_2_.7, bf16[2304]{0:T(1024)(128)(2,1)} %refs_3_.7, ...), custom_call_target="tpu_custom_call" | custom-call | tf_op jit(solution)/shard_map/step2/pallas_call | solution.py:439
  242.9 2.9 lookup.6.refs_0_
  245.9 78.1 %step3.1 = (s32[1,128]{1,0:T(1,128)}, bf16[32,2304]{1,0:T(8,128)(2,1)}, f32[2,2,16,128]{3,2,1,0:T(8,128)}, s32[1,128]{1,0:T(1,128)}) custom-call(bf16[2,16,2304]{2,1,0:T(8,128)(2,1)} %lookup.6.refs_0_, f32[2,2,16,128]{3,2,1,0:T(8,128)} %get-tuple-element.18.refs_1_, bf16[2304]{0:T(1024)(128)(2,1)} %refs_2_.7, bf16[2304]{0:T(1024)(128)(2,1)} %refs_3_.7, ...), custom_call_target="tpu_custom_call" | custom-call | tf_op jit(solution)/shard_map/step3/pallas_call | solution.py:439
  323.9 2.9 lookup.7.refs_0_
  326.8 8.9 %step4.1 = (s32[4,32]{1,0:T(4,128)}, bf16[32,2304]{1,0:T(8,128)(2,1)}) custom-call(bf16[2,16,2304]{2,1,0:T(8,128)(2,1)} %lookup.7.refs_0_, f32[2,2,16,128]{3,2,1,0:T(8,128)} %get-tuple-element.20.refs_1_, s32[1,128]{1,0:T(1,128)} %get-tuple-element.21.refs_2_, s32[1,128]{1,0:T(1,128)} %get-tuple-element.22.refs_3_, s32[1,128]{1,0:T(1,128)} %get-tuple-element.23.refs_4_), custom_call_target="tpu_custom_call" | custom-call | tf_op jit(solution)/shard_map/step4/pallas_call | solution.py:439
  335.8 1.2 copy.15
  337.0 1.6 copy.16

commit v5 on v4

--- a/solution.py
+++ b/solution.py
@@ -80,11 +80,17 @@
         n_iter = OWN + half
         width = ring.shape[1]
         inner = wg_ref.shape[1]
+        weights = [(wg_ref, 0, width), (wu_ref, width, width), (wd_ref, 2 * width, inner)]
         w_copies = [
-            pltpu.make_async_copy(wg_ref, ring.at[pl.ds(0, width)], sem_w.at[0]),
-            pltpu.make_async_copy(wu_ref, ring.at[pl.ds(width, width)], sem_w.at[1]),
-            pltpu.make_async_copy(wd_ref, ring.at[pl.ds(2 * width, inner)], sem_w.at[2]),
+            pltpu.make_async_copy(ref, ring.at[pl.ds(base, rows)], sem_w.at[k])
+            for k, (ref, base, rows) in enumerate(weights)
         ]
+
+        def w_start(k):
+            ref, base, rows = weights[k]
+            piece = rows // 9
+            for p in range(0, rows, piece):
+                pltpu.make_async_copy(ref.at[pl.ds(p, piece)], ring.at[pl.ds(base + p, piece)], sem_w.at[k]).start()
 
         def group_of(i):
             moved = jnp.where(i < HEAD + half, dp * half, half)
@@ -120,8 +126,8 @@
                 device_id_type=MESH,
             )
 
-        w_copies[0].start()
-        w_copies[1].start()
+        w_start(0)
+        w_start(1)
 
     barrier = pltpu.get_barrier_semaphore()
     peers = (sib, over) if last else (sib, over, diag, pair)
@@ -140,7 +146,7 @@
 
     if first:
         hid = hid_ref[...].astype(jnp.float32)
-        w_copies[2].start()
+        w_start(2)
         w_copies[0].wait()
         fetch_head()
     else:
@@ -151,7 +157,7 @@
         a_rows.wait()
         a_meta.wait()
         if not last:
-            w_copies[2].start()
+            w_start(2)
         mine = meta_ref[core]
         seen = meta_a[...]
         keep = mine[0] >= seen[0]

time: 339 us -> 339 us (level)
  no operation moved by 1% of the time
where the time goes in v5:
time: 339 us
  Pallas kernels  334 us (99%)
    pallas_call x5, Pallas kernels, call_step(): pl.pallas_call(functools.partial(step_kernel, (step, first, last, n_group...  323 us
    pallas_call x4, Pallas kernels, lookup(): pl.pallas_call(lookup_kernel, out_shape=jax.ShapeDtypeStruct((2, batch //...  11.6 us

profile of v5, /device:TPU:0, one launch (start us, length us, event | category | flops | bytes accessed | tf_op | source)
XLA Modules:
  0.0 338.6 jit_solution(1188735404716662254)
XLA Ops:
  1.3 79.5 %step0.1 = (f32[2,2,16,128]{3,2,1,0:T(8,128)}, s32[1,128]{1,0:T(1,128)}) custom-call(bf16[32,2304]{1,0:T(8,128)(2,1)} %refs_0_.1, bf16[2304]{0:T(1024)(128)(2,1)} %refs_2_.7, bf16[2304]{0:T(1024)(128)(2,1)} %refs_3_.7, bf16[2304]{0:T(1024)(128)(2,1)} %refs_4_.5, f32[1,1]{1,0:T(1,128)} %bitcast.1.refs_4_, bf16[2304,2304]{1,0:T(8,128)(2,1)} %refs_6_.7, ...), custom_call_target="tpu_custom_call" | custom-call | tf_op jit(solution)/shard_map/step0/pallas_call | solution.py:445
  80.8 2.9 lookup.4.refs_0_
  83.7 78.1 %step1.1 = (s32[1,128]{1,0:T(1,128)}, bf16[32,2304]{1,0:T(8,128)(2,1)}, f32[2,2,16,128]{3,2,1,0:T(8,128)}, s32[1,128]{1,0:T(1,128)}) custom-call(bf16[2,16,2304]{2,1,0:T(8,128)(2,1)} %lookup.4.refs_0_, f32[2,2,16,128]{3,2,1,0:T(8,128)} %get-tuple-element.14.refs_1_, bf16[2304]{0:T(1024)(128)(2,1)} %refs_2_.7, bf16[2304]{0:T(1024)(128)(2,1)} %refs_3_.7, ...), custom_call_target="tpu_custom_call" | custom-call | tf_op jit(solution)/shard_map/step1/pallas_call | solution.py:445
  161.8 2.9 lookup.5.refs_0_
  164.7 78.2 %step2.1 = (s32[1,128]{1,0:T(1,128)}, bf16[32,2304]{1,0:T(8,128)(2,1)}, f32[2,2,16,128]{3,2,1,0:T(8,128)}, s32[1,128]{1,0:T(1,128)}) custom-call(bf16[2,16,2304]{2,1,0:T(8,128)(2,1)} %lookup.5.refs_0_, f32[2,2,16,128]{3,2,1,0:T(8,128)} %get-tuple-element.16.refs_1_, bf16[2304]{0:T(1024)(128)(2,1)} %refs_2_.7, bf16[2304]{0:T(1024)(128)(2,1)} %refs_3_.7, ...), custom_call_target="tpu_custom_call" | custom-call | tf_op jit(solution)/shard_map/step2/pallas_call | solution.py:445
  242.9 2.9 lookup.6.refs_0_
  245.9 78.1 %step3.1 = (s32[1,128]{1,0:T(1,128)}, bf16[32,2304]{1,0:T(8,128)(2,1)}, f32[2,2,16,128]{3,2,1,0:T(8,128)}, s32[1,128]{1,0:T(1,128)}) custom-call(bf16[2,16,2304]{2,1,0:T(8,128)(2,1)} %lookup.6.refs_0_, f32[2,2,16,128]{3,2,1,0:T(8,128)} %get-tuple-element.18.refs_1_, bf16[2304]{0:T(1024)(128)(2,1)} %refs_2_.7, bf16[2304]{0:T(1024)(128)(2,1)} %refs_3_.7, ...), custom_call_target="tpu_custom_call" | custom-call | tf_op jit(solution)/shard_map/step3/pallas_call | solution.py:445
  323.9 2.9 lookup.7.refs_0_
  326.9 8.9 %step4.1 = (s32[4,32]{1,0:T(4,128)}, bf16[32,2304]{1,0:T(8,128)(2,1)}) custom-call(bf16[2,16,2304]{2,1,0:T(8,128)(2,1)} %lookup.7.refs_0_, f32[2,2,16,128]{3,2,1,0:T(8,128)} %get-tuple-element.20.refs_1_, s32[1,128]{1,0:T(1,128)} %get-tuple-element.21.refs_2_, s32[1,128]{1,0:T(1,128)} %get-tuple-element.22.refs_3_, s32[1,128]{1,0:T(1,128)} %get-tuple-element.23.refs_4_), custom_call_target="tpu_custom_call" | custom-call | tf_op jit(solution)/shard_map/step4/pallas_call | solution.py:445
  335.8 1.2 copy.15
  337.0 1.6 copy.16

commit v6 on v5

--- a/solution.py
+++ b/solution.py
@@ -19,7 +19,7 @@
 RING_GROUPS = 8
 WEIGHT_GROUPS = 6
 CUTS = ((0, 512, False), (512, 768, True))
-HEAD = 14
+HEAD = 10
 TAIL = 2
 OWN = HEAD + TAIL
 NEG = -3.0e38
@@ -50,17 +50,29 @@
     refs = list(refs)
     take = lambda n: [refs.pop(0) for _ in range(n)]
     if first:
-        (hid_ref,) = take(1)
+        (hid_hbm,) = take(1)
     else:
-        rows_ref, meta_ref = take(2)
+        rows_hbm, meta_hbm = take(2)
         if last:
             old_refs = take(step - 1)
     if not last:
-        pre_ref, post_ref, fin_ref, temp_ref, wg_ref, wu_ref, wd_ref, emb_ref, noise_ref = take(9)
+        pre_hbm, post_hbm, fin_hbm, temp_ref, wg_ref, wu_ref, wd_ref, emb_ref, noise_ref = take(9)
     if not first:
         tok_ref, hout_ref = take(2)
     if not last:
         best_ref, line_ref = take(2)
+    if first:
+        hid_ref, sem_in = take(2)
+        inputs = [(hid_hbm, hid_ref)]
+    else:
+        rows_ref, meta_ref, sem_in = take(3)
+        inputs = [(rows_hbm, rows_ref), (meta_hbm, meta_ref)]
+    if not last:
+        pre_ref, post_ref, fin_ref, sem_gain = take(4)
+        gains = [(pre_hbm, pre_ref), (post_hbm, post_ref), (fin_hbm, fin_ref)]
+    in_copies = [pltpu.make_async_copy(src, dst, sem_in.at[k]) for k, (src, dst) in enumerate(inputs)]
+    for copy in in_copies:
+        copy.start()
     if not first:
         rows_a, meta_a, rows_m, meta_m, rows_b, meta_b, rows_f, meta_f, rows_c, meta_c, sem_rows, sem_meta = take(12)
     if not last:
@@ -126,6 +138,9 @@
                 device_id_type=MESH,
             )
 
+        gain_copies = [pltpu.make_async_copy(src, dst, sem_gain.at[k]) for k, (src, dst) in enumerate(gains)]
+        for copy in gain_copies:
+            copy.start()
         w_start(0)
         w_start(1)
 
@@ -144,6 +159,8 @@
         early = 6
         pl.loop(0, early)(lambda j: nr_copy(j).start())
 
+    for copy in in_copies:
+        copy.wait()
     if first:
         hid = hid_ref[...].astype(jnp.float32)
         w_start(2)
@@ -207,6 +224,8 @@
     batch = hid.shape[0]
     quarter = batch // 4
     hid32[...] = hid.reshape(4, quarter, width)
+    for copy in gain_copies:
+        copy.wait()
     normed = rms_scale(hid, gain(pre_ref)).astype(jnp.bfloat16)
     f_two[pl.ds(0, batch)] = normed
     w_copies[1].wait()
@@ -397,10 +416,16 @@
     half = (n_group - OWN) // 2
     n_iter = OWN + half
     hb, quarter = batch // 2, batch // 4
-    in_specs = [vmem] * (1 if first else 2 + (step - 1) * last)
-    if not last:
-        in_specs += [vmem] * 3 + [pl.BlockSpec(memory_space=pltpu.SMEM)] + [hbm] * 5
+    in_specs = [hbm] * (1 if first else 2) + [vmem] * ((step - 1) * last)
+    if not last:
+        in_specs += [hbm] * 3 + [pl.BlockSpec(memory_space=pltpu.SMEM)] + [hbm] * 5
     outs, scratch = [], []
+    if first:
+        scratch += [pltpu.VMEM((batch, width), bf16), dma((1,))]
+    else:
+        scratch += [pltpu.VMEM((2, hb, width), bf16), pltpu.VMEM((2, 2, hb, 128), f32), dma((2,))]
+    if not last:
+        scratch += [pltpu.VMEM((width,), bf16)] * 3 + [dma((3,))]
     if not first:
         outs += [jax.ShapeDtypeStruct((steps, batch) if last else (1, 128), i32), jax.ShapeDtypeStruct((batch, width), bf16)]
         rows, meta = pltpu.VMEM((hb, width), bf16), pltpu.VMEM((2, hb, 128), f32)

time: 339 us -> 342 us (level)
  no operation moved by 1% of the time
where the time goes in v6:
time: 342 us; the launch traced here: 341 us
  Pallas kernels  337 us (99%)
    pallas_call x5, Pallas kernels, call_step(): pl.pallas_call(functools.partial(step_kernel, (step, first, last, n_group...  325 us
    pallas_call x4, Pallas kernels, lookup(): pl.pallas_call(lookup_kernel, out_shape=jax.ShapeDtypeStruct((2, batch //...  11.6 us

profile of v6, /device:TPU:0, one launch (start us, length us, event | category | flops | bytes accessed | tf_op | source)
XLA Modules:
  0.0 341.2 jit_solution(15999558981625306279)
XLA Ops:
  1.3 79.9 %step0.1 = (f32[2,2,16,128]{3,2,1,0:T(8,128)}, s32[1,128]{1,0:T(1,128)}) custom-call(bf16[32,2304]{1,0:T(8,128)(2,1)} %refs_0_.1, bf16[2304]{0:T(1024)(128)(2,1)} %refs_2_.7, bf16[2304]{0:T(1024)(128)(2,1)} %refs_3_.7, bf16[2304]{0:T(1024)(128)(2,1)} %refs_4_.5, f32[1,1]{1,0:T(1,128)} %bitcast.1.refs_4_, bf16[2304,2304]{1,0:T(8,128)(2,1)} %refs_6_.7, ...), custom_call_target="tpu_custom_call" | custom-call | tf_op jit(solution)/shard_map/step0/pallas_call | solution.py:470
  81.2 2.9 lookup.4.refs_0_
  84.1 78.7 %step1.1 = (s32[1,128]{1,0:T(1,128)}, bf16[32,2304]{1,0:T(8,128)(2,1)}, f32[2,2,16,128]{3,2,1,0:T(8,128)}, s32[1,128]{1,0:T(1,128)}) custom-call(bf16[2,16,2304]{2,1,0:T(8,128)(2,1)} %lookup.4.refs_0_, f32[2,2,16,128]{3,2,1,0:T(8,128)} %get-tuple-element.14.refs_1_, bf16[2304]{0:T(1024)(128)(2,1)} %refs_2_.7, bf16[2304]{0:T(1024)(128)(2,1)} %refs_3_.7, ...), custom_call_target="tpu_custom_call" | custom-call | tf_op jit(solution)/shard_map/step1/pallas_call | solution.py:470
  162.8 2.9 lookup.5.refs_0_
  165.7 79.3 %step2.1 = (s32[1,128]{1,0:T(1,128)}, bf16[32,2304]{1,0:T(8,128)(2,1)}, f32[2,2,16,128]{3,2,1,0:T(8,128)}, s32[1,128]{1,0:T(1,128)}) custom-call(bf16[2,16,2304]{2,1,0:T(8,128)(2,1)} %lookup.5.refs_0_, f32[2,2,16,128]{3,2,1,0:T(8,128)} %get-tuple-element.16.refs_1_, bf16[2304]{0:T(1024)(128)(2,1)} %refs_2_.7, bf16[2304]{0:T(1024)(128)(2,1)} %refs_3_.7, ...), custom_call_target="tpu_custom_call" | custom-call | tf_op jit(solution)/shard_map/step2/pallas_call | solution.py:470
  245.1 2.9 lookup.6.refs_0_
  248.0 78.7 %step3.1 = (s32[1,128]{1,0:T(1,128)}, bf16[32,2304]{1,0:T(8,128)(2,1)}, f32[2,2,16,128]{3,2,1,0:T(8,128)}, s32[1,128]{1,0:T(1,128)}) custom-call(bf16[2,16,2304]{2,1,0:T(8,128)(2,1)} %lookup.6.refs_0_, f32[2,2,16,128]{3,2,1,0:T(8,128)} %get-tuple-element.18.refs_1_, bf16[2304]{0:T(1024)(128)(2,1)} %refs_2_.7, bf16[2304]{0:T(1024)(128)(2,1)} %refs_3_.7, ...), custom_call_target="tpu_custom_call" | custom-call | tf_op jit(solution)/shard_map/step3/pallas_call | solution.py:470
  326.7 2.9 lookup.7.refs_0_
  329.6 8.7 %step4.1 = (s32[4,32]{1,0:T(4,128)}, bf16[32,2304]{1,0:T(8,128)(2,1)}) custom-call(bf16[2,16,2304]{2,1,0:T(8,128)(2,1)} %lookup.7.refs_0_, f32[2,2,16,128]{3,2,1,0:T(8,128)} %get-tuple-element.20.refs_1_, s32[1,128]{1,0:T(1,128)} %get-tuple-element.21.refs_2_, s32[1,128]{1,0:T(1,128)} %get-tuple-element.22.refs_3_, s32[1,128]{1,0:T(1,128)} %get-tuple-element.23.refs_4_), custom_call_target="tpu_custom_call" | custom-call | tf_op jit(solution)/shard_map/step4/pallas_call | solution.py:470
  338.3 1.2 copy.15
  339.6 1.6 copy.16

commit v7 on v6

--- a/solution.py
+++ b/solution.py
@@ -17,9 +17,10 @@
 NSUB = 2
 GROUP = SUB * NSUB
 RING_GROUPS = 8
+SPREAD = 3
 WEIGHT_GROUPS = 6
 CUTS = ((0, 512, False), (512, 768, True))
-HEAD = 10
+HEAD = 12
 TAIL = 2
 OWN = HEAD + TAIL
 NEG = -3.0e38
@@ -288,10 +289,7 @@
         return jnp.concatenate(order, axis=0).astype(jnp.bfloat16)
 
     f_two[pl.ds(0, batch)] = in_order(f_send, f_all)
-    f_pair_copy.wait()
     g_copies = [remote(f_pair, g_all.at[k], sem_g.at[k], peer) for k, peer in enumerate((sib, over, diag))]
-    for copy in g_copies:
-        copy.start()
 
     bv[...] = jnp.full_like(bv, NEG)
     bi[...] = jnp.zeros_like(bi)
@@ -332,6 +330,12 @@
     def own(i):
         no_copy(i).wait()
         score(i, batch, [nz_own.at[i]])
+
+        @pl.when(i == SPREAD)
+        def _():
+            f_pair_copy.wait()
+            for copy in g_copies:
+                copy.start()
 
     def shared(i):
         no_copy(i).wait()

time: 342 us -> 336 us (0.982)
  Pallas kernels: 337 us -> 332 us
    pallas_call x5, Pallas kernels: 325 us -> 320 us  [call_step(): pl.pallas_call(functools.partial(step_kernel, (step, first, last, n_group...]
where the time goes in v7:
time: 336 us
  Pallas kernels  332 us (99%)
    pallas_call x5, Pallas kernels, call_step(): pl.pallas_call(functools.partial(step_kernel, (step, first, last, n_group...  320 us
    pallas_call x4, Pallas kernels, lookup(): pl.pallas_call(lookup_kernel, out_shape=jax.ShapeDtypeStruct((2, batch //...  11.6 us

profile of v7, /device:TPU:0, one launch (start us, length us, event | category | flops | bytes accessed | tf_op | source)
XLA Modules:
  0.0 335.7 jit_solution(17293271882208696893)
XLA Ops:
  1.3 76.4 %step0.1 = (f32[2,2,16,128]{3,2,1,0:T(8,128)}, s32[1,128]{1,0:T(1,128)}) custom-call(bf16[32,2304]{1,0:T(8,128)(2,1)} %refs_0_.1, bf16[2304]{0:T(1024)(128)(2,1)} %refs_2_.7, bf16[2304]{0:T(1024)(128)(2,1)} %refs_3_.7, bf16[2304]{0:T(1024)(128)(2,1)} %refs_4_.5, f32[1,1]{1,0:T(1,128)} %bitcast.1.refs_4_, bf16[2304,2304]{1,0:T(8,128)(2,1)} %refs_6_.7, ...), custom_call_target="tpu_custom_call" | custom-call | tf_op jit(solution)/shard_map/step0/pallas_call | solution.py:474
  77.7 2.9 lookup.4.refs_0_
  80.6 77.6 %step1.1 = (s32[1,128]{1,0:T(1,128)}, bf16[32,2304]{1,0:T(8,128)(2,1)}, f32[2,2,16,128]{3,2,1,0:T(8,128)}, s32[1,128]{1,0:T(1,128)}) custom-call(bf16[2,16,2304]{2,1,0:T(8,128)(2,1)} %lookup.4.refs_0_, f32[2,2,16,128]{3,2,1,0:T(8,128)} %get-tuple-element.14.refs_1_, bf16[2304]{0:T(1024)(128)(2,1)} %refs_2_.7, bf16[2304]{0:T(1024)(128)(2,1)} %refs_3_.7, ...), custom_call_target="tpu_custom_call" | custom-call | tf_op jit(solution)/shard_map/step1/pallas_call | solution.py:474
  158.2 2.9 lookup.5.refs_0_
  161.1 78.9 %step2.1 = (s32[1,128]{1,0:T(1,128)}, bf16[32,2304]{1,0:T(8,128)(2,1)}, f32[2,2,16,128]{3,2,1,0:T(8,128)}, s32[1,128]{1,0:T(1,128)}) custom-call(bf16[2,16,2304]{2,1,0:T(8,128)(2,1)} %lookup.5.refs_0_, f32[2,2,16,128]{3,2,1,0:T(8,128)} %get-tuple-element.16.refs_1_, bf16[2304]{0:T(1024)(128)(2,1)} %refs_2_.7, bf16[2304]{0:T(1024)(128)(2,1)} %refs_3_.7, ...), custom_call_target="tpu_custom_call" | custom-call | tf_op jit(solution)/shard_map/step2/pallas_call | solution.py:474
  240.1 2.9 lookup.6.refs_0_
  243.0 77.8 %step3.1 = (s32[1,128]{1,0:T(1,128)}, bf16[32,2304]{1,0:T(8,128)(2,1)}, f32[2,2,16,128]{3,2,1,0:T(8,128)}, s32[1,128]{1,0:T(1,128)}) custom-call(bf16[2,16,2304]{2,1,0:T(8,128)(2,1)} %lookup.6.refs_0_, f32[2,2,16,128]{3,2,1,0:T(8,128)} %get-tuple-element.18.refs_1_, bf16[2304]{0:T(1024)(128)(2,1)} %refs_2_.7, bf16[2304]{0:T(1024)(128)(2,1)} %refs_3_.7, ...), custom_call_target="tpu_custom_call" | custom-call | tf_op jit(solution)/shard_map/step3/pallas_call | solution.py:474
  320.8 2.9 lookup.7.refs_0_
  323.7 9.2 %step4.1 = (s32[4,32]{1,0:T(4,128)}, bf16[32,2304]{1,0:T(8,128)(2,1)}) custom-call(bf16[2,16,2304]{2,1,0:T(8,128)(2,1)} %lookup.7.refs_0_, f32[2,2,16,128]{3,2,1,0:T(8,128)} %get-tuple-element.20.refs_1_, s32[1,128]{1,0:T(1,128)} %get-tuple-element.21.refs_2_, s32[1,128]{1,0:T(1,128)} %get-tuple-element.22.refs_3_, s32[1,128]{1,0:T(1,128)} %get-tuple-element.23.refs_4_), custom_call_target="tpu_custom_call" | custom-call | tf_op jit(solution)/shard_map/step4/pallas_call | solution.py:474
  332.9 1.2 copy.15
  334.2 1.6 copy.16

commit v8 on v7

--- a/solution.py
+++ b/solution.py
@@ -16,7 +16,7 @@
 SUB = 640
 NSUB = 2
 GROUP = SUB * NSUB
-RING_GROUPS = 8
+RING_GROUPS = 9
 SPREAD = 3
 WEIGHT_GROUPS = 6
 CUTS = ((0, 512, False), (512, 768, True))
@@ -121,11 +121,12 @@
         def e_start(i):
             for j in range(NSUB):
                 e_copy(i, j).start()
+            no_copy(i).start()
 
         def no_copy(i):
             group = group_of(i)
             return pltpu.make_async_copy(
-                noise_ref.at[step, :, pl.ds(group * GROUP, GROUP)], nz_own.at[i], sem_no.at[i]
+                noise_ref.at[step, :, pl.ds(group * GROUP, GROUP)], nz_own.at[lax.rem(i, RING_GROUPS)], sem_no.at[lax.rem(i, RING_GROUPS)]
             )
 
         def nr_copy(j):
@@ -152,9 +153,8 @@
     pl.semaphore_wait(barrier, len(peers))
 
     def fetch_head():
-        e_start(0)
-        e_start(1)
-        pl.loop(0, n_iter)(lambda i: no_copy(i).start())
+        for i in range(RING_GROUPS - WEIGHT_GROUPS):
+            e_start(i)
 
     if not last:
         early = 6
@@ -164,8 +164,8 @@
         copy.wait()
     if first:
         hid = hid_ref[...].astype(jnp.float32)
+        w_copies[0].wait()
         w_start(2)
-        w_copies[0].wait()
         fetch_head()
     else:
         a_rows = remote(rows_ref.at[1 - core], rows_a, sem_rows.at[0], sib)
@@ -174,8 +174,6 @@
         a_meta.start()
         a_rows.wait()
         a_meta.wait()
-        if not last:
-            w_start(2)
         mine = meta_ref[core]
         seen = meta_a[...]
         keep = mine[0] >= seen[0]
@@ -189,6 +187,8 @@
         b_meta.start()
         b_rows.wait()
         b_meta.wait()
+        if not last:
+            w_start(2)
         mine = meta_m[...]
         seen = meta_b[...]
         keep = mine[0] >= seen[0]
@@ -240,7 +240,8 @@
         up = jnp.dot(lhs, ring[pl.ds(width, width), cols], preferred_element_type=jnp.float32)
         gate_s[:, cols] = (jax.nn.gelu(gate, approximate=True) * up).astype(jnp.bfloat16)
 
-    for i in range(2, 2 + (2 * width) // GROUP):
+    free = RING_GROUPS - WEIGHT_GROUPS + (2 * width) // GROUP
+    for i in range(RING_GROUPS - WEIGHT_GROUPS, free):
         e_start(i)
     w_copies[2].wait()
 
@@ -251,7 +252,7 @@
             gate_s[...], ring[pl.ds(2 * width, inner), cols], preferred_element_type=jnp.float32
         ).reshape(4, quarter, col)
 
-    for i in range(2 + (2 * width) // GROUP, RING_GROUPS):
+    for i in range(free, RING_GROUPS):
         e_start(i)
 
     ra = remote(part_s.at[pl.ds(2 * (1 - core), 2)], part_a, sem_ra, sib)
@@ -329,7 +330,7 @@
 
     def own(i):
         no_copy(i).wait()
-        score(i, batch, [nz_own.at[i]])
+        score(i, batch, [nz_own.at[lax.rem(i, RING_GROUPS)]])
 
         @pl.when(i == SPREAD)
         def _():
@@ -340,7 +341,7 @@
     def shared(i):
         no_copy(i).wait()
         nr_copy(i - HEAD).wait_recv()
-        score(i, 2 * batch, [nz_own.at[i], nz_oth.at[i - HEAD]])
+        score(i, 2 * batch, [nz_own.at[lax.rem(i, RING_GROUPS)], nz_oth.at[i - HEAD]])
 
     def settle(part):
         val = bv[pl.ds(part * batch, batch)]
@@ -441,7 +442,7 @@
         ]
         scratch += [
             pltpu.VMEM((RING_GROUPS * GROUP, width), bf16),
-            pltpu.VMEM((n_iter, batch, GROUP), f32),
+            pltpu.VMEM((RING_GROUPS, batch, GROUP), f32),
             pltpu.VMEM((half, batch, GROUP), f32),
             pltpu.VMEM((4, quarter, width), f32),
             pltpu.VMEM((2, quarter, width), f32),
@@ -461,7 +462,7 @@
             pltpu.VMEM((2, batch, 128), f32),
             dma((3,)),
             dma((RING_GROUPS, NSUB)),
-            dma((n_iter,)),
+            dma((RING_GROUPS,)),
             dma((half,)),
             dma((half,)),
             dma((2,)),

time: 336 us -> 336 us (level)
  no operation moved by 1% of the time
where the time goes in v8:
time: 336 us
  Pallas kernels  331 us (99%)
    pallas_call x5, Pallas kernels, call_step(): pl.pallas_call(functools.partial(step_kernel, (step, first, last, n_group...  320 us
    pallas_call x4, Pallas kernels, lookup(): pl.pallas_call(lookup_kernel, out_shape=jax.ShapeDtypeStruct((2, batch //...  11.6 us

profile of v8, /device:TPU:0, one launch (start us, length us, event | category | flops | bytes accessed | tf_op | source)
XLA Modules:
  0.0 335.6 jit_solution(2863204719520693503)
XLA Ops:
  1.3 76.2 %step0.1 = (f32[2,2,16,128]{3,2,1,0:T(8,128)}, s32[1,128]{1,0:T(1,128)}) custom-call(bf16[32,2304]{1,0:T(8,128)(2,1)} %refs_0_.1, bf16[2304]{0:T(1024)(128)(2,1)} %refs_2_.7, bf16[2304]{0:T(1024)(128)(2,1)} %refs_3_.7, bf16[2304]{0:T(1024)(128)(2,1)} %refs_4_.5, f32[1,1]{1,0:T(1,128)} %bitcast.1.refs_4_, bf16[2304,2304]{1,0:T(8,128)(2,1)} %refs_6_.7, ...), custom_call_target="tpu_custom_call" | custom-call | tf_op jit(solution)/shard_map/step0/pallas_call | solution.py:475
  77.5 2.9 lookup.4.refs_0_
  80.4 77.6 %step1.1 = (s32[1,128]{1,0:T(1,128)}, bf16[32,2304]{1,0:T(8,128)(2,1)}, f32[2,2,16,128]{3,2,1,0:T(8,128)}, s32[1,128]{1,0:T(1,128)}) custom-call(bf16[2,16,2304]{2,1,0:T(8,128)(2,1)} %lookup.4.refs_0_, f32[2,2,16,128]{3,2,1,0:T(8,128)} %get-tuple-element.14.refs_1_, bf16[2304]{0:T(1024)(128)(2,1)} %refs_2_.7, bf16[2304]{0:T(1024)(128)(2,1)} %refs_3_.7, ...), custom_call_target="tpu_custom_call" | custom-call | tf_op jit(solution)/shard_map/step1/pallas_call | solution.py:475
  158.1 2.9 lookup.5.refs_0_
  161.0 78.9 %step2.1 = (s32[1,128]{1,0:T(1,128)}, bf16[32,2304]{1,0:T(8,128)(2,1)}, f32[2,2,16,128]{3,2,1,0:T(8,128)}, s32[1,128]{1,0:T(1,128)}) custom-call(bf16[2,16,2304]{2,1,0:T(8,128)(2,1)} %lookup.5.refs_0_, f32[2,2,16,128]{3,2,1,0:T(8,128)} %get-tuple-element.16.refs_1_, bf16[2304]{0:T(1024)(128)(2,1)} %refs_2_.7, bf16[2304]{0:T(1024)(128)(2,1)} %refs_3_.7, ...), custom_call_target="tpu_custom_call" | custom-call | tf_op jit(solution)/shard_map/step2/pallas_call | solution.py:475
  239.9 2.9 lookup.6.refs_0_
  242.8 77.8 %step3.1 = (s32[1,128]{1,0:T(1,128)}, bf16[32,2304]{1,0:T(8,128)(2,1)}, f32[2,2,16,128]{3,2,1,0:T(8,128)}, s32[1,128]{1,0:T(1,128)}) custom-call(bf16[2,16,2304]{2,1,0:T(8,128)(2,1)} %lookup.6.refs_0_, f32[2,2,16,128]{3,2,1,0:T(8,128)} %get-tuple-element.18.refs_1_, bf16[2304]{0:T(1024)(128)(2,1)} %refs_2_.7, bf16[2304]{0:T(1024)(128)(2,1)} %refs_3_.7, ...), custom_call_target="tpu_custom_call" | custom-call | tf_op jit(solution)/shard_map/step3/pallas_call | solution.py:475
  320.6 2.9 lookup.7.refs_0_
  323.5 9.2 %step4.1 = (s32[4,32]{1,0:T(4,128)}, bf16[32,2304]{1,0:T(8,128)(2,1)}) custom-call(bf16[2,16,2304]{2,1,0:T(8,128)(2,1)} %lookup.7.refs_0_, f32[2,2,16,128]{3,2,1,0:T(8,128)} %get-tuple-element.20.refs_1_, s32[1,128]{1,0:T(1,128)} %get-tuple-element.21.refs_2_, s32[1,128]{1,0:T(1,128)} %get-tuple-element.22.refs_3_, s32[1,128]{1,0:T(1,128)} %get-tuple-element.23.refs_4_), custom_call_target="tpu_custom_call" | custom-call | tf_op jit(solution)/shard_map/step4/pallas_call | solution.py:475
  332.8 1.2 copy.15
  334.0 1.6 copy.16

commit v9 on v8

--- a/solution.py
+++ b/solution.py
@@ -20,8 +20,8 @@
 SPREAD = 3
 WEIGHT_GROUPS = 6
 CUTS = ((0, 512, False), (512, 768, True))
-HEAD = 12
-TAIL = 2
+HEAD = 15
+TAIL = 1
 OWN = HEAD + TAIL
 NEG = -3.0e38
 

time: 336 us -> 345 us (1.027)
  Pallas kernels: 331 us -> 340 us
    pallas_call x5, Pallas kernels: 320 us -> 328 us  [call_step(): pl.pallas_call(functools.partial(step_kernel, (step, first, last, n_group...]
where the time goes in v9:
time: 345 us; the launch traced here: 344 us
  Pallas kernels  340 us (99%)
    pallas_call x5, Pallas kernels, call_step(): pl.pallas_call(functools.partial(step_kernel, (step, first, last, n_group...  328 us
    pallas_call x4, Pallas kernels, lookup(): pl.pallas_call(lookup_kernel, out_shape=jax.ShapeDtypeStruct((2, batch //...  11.6 us

profile of v9, /device:TPU:0, one launch (start us, length us, event | category | flops | bytes accessed | tf_op | source)
XLA Modules:
  0.0 344.1 jit_solution(11846486742278583930)
XLA Ops:
  1.3 76.8 %step0.1 = (f32[2,2,16,128]{3,2,1,0:T(8,128)}, s32[1,128]{1,0:T(1,128)}) custom-call(bf16[32,2304]{1,0:T(8,128)(2,1)} %refs_0_.1, bf16[2304]{0:T(1024)(128)(2,1)} %refs_2_.7, bf16[2304]{0:T(1024)(128)(2,1)} %refs_3_.7, bf16[2304]{0:T(1024)(128)(2,1)} %refs_4_.5, f32[1,1]{1,0:T(1,128)} %bitcast.1.refs_4_, bf16[2304,2304]{1,0:T(8,128)(2,1)} %refs_6_.7, ...), custom_call_target="tpu_custom_call" | custom-call | tf_op jit(solution)/shard_map/step0/pallas_call | solution.py:475
  78.1 2.9 lookup.4.refs_0_
  81.0 80.9 %step1.1 = (s32[1,128]{1,0:T(1,128)}, bf16[32,2304]{1,0:T(8,128)(2,1)}, f32[2,2,16,128]{3,2,1,0:T(8,128)}, s32[1,128]{1,0:T(1,128)}) custom-call(bf16[2,16,2304]{2,1,0:T(8,128)(2,1)} %lookup.4.refs_0_, f32[2,2,16,128]{3,2,1,0:T(8,128)} %get-tuple-element.14.refs_1_, bf16[2304]{0:T(1024)(128)(2,1)} %refs_2_.7, bf16[2304]{0:T(1024)(128)(2,1)} %refs_3_.7, ...), custom_call_target="tpu_custom_call" | custom-call | tf_op jit(solution)/shard_map/step1/pallas_call | solution.py:475
  161.9 2.9 lookup.5.refs_0_
  164.8 81.1 %step2.1 = (s32[1,128]{1,0:T(1,128)}, bf16[32,2304]{1,0:T(8,128)(2,1)}, f32[2,2,16,128]{3,2,1,0:T(8,128)}, s32[1,128]{1,0:T(1,128)}) custom-call(bf16[2,16,2304]{2,1,0:T(8,128)(2,1)} %lookup.5.refs_0_, f32[2,2,16,128]{3,2,1,0:T(8,128)} %get-tuple-element.16.refs_1_, bf16[2304]{0:T(1024)(128)(2,1)} %refs_2_.7, bf16[2304]{0:T(1024)(128)(2,1)} %refs_3_.7, ...), custom_call_target="tpu_custom_call" | custom-call | tf_op jit(solution)/shard_map/step2/pallas_call | solution.py:475
  245.9 2.9 lookup.6.refs_0_
  248.8 80.9 %step3.1 = (s32[1,128]{1,0:T(1,128)}, bf16[32,2304]{1,0:T(8,128)(2,1)}, f32[2,2,16,128]{3,2,1,0:T(8,128)}, s32[1,128]{1,0:T(1,128)}) custom-call(bf16[2,16,2304]{2,1,0:T(8,128)(2,1)} %lookup.6.refs_0_, f32[2,2,16,128]{3,2,1,0:T(8,128)} %get-tuple-element.18.refs_1_, bf16[2304]{0:T(1024)(128)(2,1)} %refs_2_.7, bf16[2304]{0:T(1024)(128)(2,1)} %refs_3_.7, ...), custom_call_target="tpu_custom_call" | custom-call | tf_op jit(solution)/shard_map/step3/pallas_call | solution.py:475
  329.6 2.9 lookup.7.refs_0_
  332.6 8.7 %step4.1 = (s32[4,32]{1,0:T(4,128)}, bf16[32,2304]{1,0:T(8,128)(2,1)}) custom-call(bf16[2,16,2304]{2,1,0:T(8,128)(2,1)} %lookup.7.refs_0_, f32[2,2,16,128]{3,2,1,0:T(8,128)} %get-tuple-element.20.refs_1_, s32[1,128]{1,0:T(1,128)} %get-tuple-element.21.refs_2_, s32[1,128]{1,0:T(1,128)} %get-tuple-element.22.refs_3_, s32[1,128]{1,0:T(1,128)} %get-tuple-element.23.refs_4_), custom_call_target="tpu_custom_call" | custom-call | tf_op jit(solution)/shard_map/step4/pallas_call | solution.py:475
  341.3 1.2 copy.15
  342.5 1.6 copy.16

commit v10 on v8

--- a/solution.py
+++ b/solution.py
@@ -17,7 +17,7 @@
 NSUB = 2
 GROUP = SUB * NSUB
 RING_GROUPS = 9
-SPREAD = 3
+SPREAD = 5
 WEIGHT_GROUPS = 6
 CUTS = ((0, 512, False), (512, 768, True))
 HEAD = 12
@@ -157,7 +157,7 @@
             e_start(i)
 
     if not last:
-        early = 6
+        early = 7
         pl.loop(0, early)(lambda j: nr_copy(j).start())
 
     for copy in in_copies:
@@ -174,6 +174,8 @@
         a_meta.start()
         a_rows.wait()
         a_meta.wait()
+        if not last:
+            w_start(2)
         mine = meta_ref[core]
         seen = meta_a[...]
         keep = mine[0] >= seen[0]
@@ -188,7 +190,7 @@
         b_rows.wait()
         b_meta.wait()
         if not last:
-            w_start(2)
+            fetch_head()
         mine = meta_m[...]
         seen = meta_b[...]
         keep = mine[0] >= seen[0]
@@ -204,7 +206,6 @@
         c_meta.wait()
         if not last:
             w_copies[0].wait()
-            fetch_head()
         low = core == 0
         r_f, r_c = rows_f[...].astype(jnp.float32), rows_c[...].astype(jnp.float32)
         t_f, t_c = meta_f[1], meta_c[1]

time: 336 us -> 336 us (level)
  no operation moved by 1% of the time
where the time goes in v10:
time: 336 us; the launch traced here: 335 us
  Pallas kernels  331 us (99%)
    pallas_call x5, Pallas kernels, call_step(): pl.pallas_call(functools.partial(step_kernel, (step, first, last, n_group...  319 us
    pallas_call x4, Pallas kernels, lookup(): pl.pallas_call(lookup_kernel, out_shape=jax.ShapeDtypeStruct((2, batch //...  11.6 us

profile of v10, /device:TPU:0, one launch (start us, length us, event | category | flops | bytes accessed | tf_op | source)
XLA Modules:
  0.0 335.1 jit_solution(15864527825964539106)
XLA Ops:
  1.3 76.2 %step0.1 = (f32[2,2,16,128]{3,2,1,0:T(8,128)}, s32[1,128]{1,0:T(1,128)}) custom-call(bf16[32,2304]{1,0:T(8,128)(2,1)} %refs_0_.1, bf16[2304]{0:T(1024)(128)(2,1)} %refs_2_.7, bf16[2304]{0:T(1024)(128)(2,1)} %refs_3_.7, bf16[2304]{0:T(1024)(128)(2,1)} %refs_4_.5, f32[1,1]{1,0:T(1,128)} %bitcast.1.refs_4_, bf16[2304,2304]{1,0:T(8,128)(2,1)} %refs_6_.7, ...), custom_call_target="tpu_custom_call" | custom-call | tf_op jit(solution)/shard_map/step0/pallas_call | solution.py:476
  77.5 2.9 lookup.4.refs_0_
  80.4 77.5 %step1.1 = (s32[1,128]{1,0:T(1,128)}, bf16[32,2304]{1,0:T(8,128)(2,1)}, f32[2,2,16,128]{3,2,1,0:T(8,128)}, s32[1,128]{1,0:T(1,128)}) custom-call(bf16[2,16,2304]{2,1,0:T(8,128)(2,1)} %lookup.4.refs_0_, f32[2,2,16,128]{3,2,1,0:T(8,128)} %get-tuple-element.14.refs_1_, bf16[2304]{0:T(1024)(128)(2,1)} %refs_2_.7, bf16[2304]{0:T(1024)(128)(2,1)} %refs_3_.7, ...), custom_call_target="tpu_custom_call" | custom-call | tf_op jit(solution)/shard_map/step1/pallas_call | solution.py:476
  157.9 2.9 lookup.5.refs_0_
  160.8 78.8 %step2.1 = (s32[1,128]{1,0:T(1,128)}, bf16[32,2304]{1,0:T(8,128)(2,1)}, f32[2,2,16,128]{3,2,1,0:T(8,128)}, s32[1,128]{1,0:T(1,128)}) custom-call(bf16[2,16,2304]{2,1,0:T(8,128)(2,1)} %lookup.5.refs_0_, f32[2,2,16,128]{3,2,1,0:T(8,128)} %get-tuple-element.16.refs_1_, bf16[2304]{0:T(1024)(128)(2,1)} %refs_2_.7, bf16[2304]{0:T(1024)(128)(2,1)} %refs_3_.7, ...), custom_call_target="tpu_custom_call" | custom-call | tf_op jit(solution)/shard_map/step2/pallas_call | solution.py:476
  239.6 2.9 lookup.6.refs_0_
  242.5 77.6 %step3.1 = (s32[1,128]{1,0:T(1,128)}, bf16[32,2304]{1,0:T(8,128)(2,1)}, f32[2,2,16,128]{3,2,1,0:T(8,128)}, s32[1,128]{1,0:T(1,128)}) custom-call(bf16[2,16,2304]{2,1,0:T(8,128)(2,1)} %lookup.6.refs_0_, f32[2,2,16,128]{3,2,1,0:T(8,128)} %get-tuple-element.18.refs_1_, bf16[2304]{0:T(1024)(128)(2,1)} %refs_2_.7, bf16[2304]{0:T(1024)(128)(2,1)} %refs_3_.7, ...), custom_call_target="tpu_custom_call" | custom-call | tf_op jit(solution)/shard_map/step3/pallas_call | solution.py:476
  320.1 2.9 lookup.7.refs_0_
  323.0 9.2 %step4.1 = (s32[4,32]{1,0:T(4,128)}, bf16[32,2304]{1,0:T(8,128)(2,1)}) custom-call(bf16[2,16,2304]{2,1,0:T(8,128)(2,1)} %lookup.7.refs_0_, f32[2,2,16,128]{3,2,1,0:T(8,128)} %get-tuple-element.20.refs_1_, s32[1,128]{1,0:T(1,128)} %get-tuple-element.21.refs_2_, s32[1,128]{1,0:T(1,128)} %get-tuple-element.22.refs_3_, s32[1,128]{1,0:T(1,128)} %get-tuple-element.23.refs_4_), custom_call_target="tpu_custom_call" | custom-call | tf_op jit(solution)/shard_map/step4/pallas_call | solution.py:476
  332.3 1.2 copy.15
  333.5 1.6 copy.16
